TPU v7x, 256 devices: a whole 4x4x8 slice. The times are simulated.
256 devices in a mesh: dp: 8 (over x_lo, y), mp: 32 (over z, x_hi, core).
Axes of the slice: x: 4 (x_hi: 2, x_lo: 2; x = x_hi * 2 + x_lo), y: 4, z: 8, core: 2. Of those that a mesh axis runs over, the one named last changes fastest.
Arguments:
- tokens: bfloat16 [1024, 6144], P(('dp', 'mp')), may hold values from -6 to 6
- norm_gain: float32 [6144], replicated, may hold values from 0.5 to 1.5
- w_query: bfloat16 [6144, 4096], P('dp', 'mp'), as said below
- w_key: bfloat16 [6144, 4096], P('dp', 'mp'), as said below
- w_value: bfloat16 [6144, 4096], P('dp', 'mp'), may hold values from -0.078125 to 0.078125
- w_inner: bfloat16 [6144, 24576], P('dp', 'mp'), may hold values from -0.078125 to 0.078125
- bias_inner: float32 [24576], P('mp'), may hold values from -3 to 3
- w_attn_out: bfloat16 [4096, 6144], P('mp', 'dp'), may hold values from -0.09375 to 0.09375
- w_outer: bfloat16 [24576, 6144], P('mp', 'dp'), may hold values from -0.0390625 to 0.0390625
- temper: float32 [32], P('mp'), may hold values from 0.5 to 24
Outputs:
- result: bfloat16 [1024, 6144], P(('dp', 'mp'))
Inputs may be any that keep to these rules, and one draw needn't show every extreme that they name: `w_query`: entries of order 6144 ** -0.5. `w_key`: entries of order 6144 ** -0.5.
All inputs are finite; a program needn't handle non-finite values.
Results may differ from a plain program's by a relative error of at most 0.023.
Values may be sent and summed in bfloat16 or wider, within the bound.
A program may use at most 64 MiB of HBM per device.

v0:
```python
import math

import jax
import jax.numpy as jnp
from jax import lax
from jax.sharding import Mesh
from jax.sharding import PartitionSpec as P

HEAD = 128
MP = ("mp_0", "mp_1", "mp_2")
DP_MP = ("dp", "mp_0", "mp_1", "mp_2")


def copy_for_each(shard, axis):
    copies = jnp.broadcast_to(shard, (lax.axis_size(axis), *shard.shape))
    return lax.all_to_all(copies, axis, split_axis=0, concat_axis=0, tiled=True)


def laid_out(tiles, dim):
    shape = list(tiles.shape[1:])
    shape[dim] *= tiles.shape[0]
    return jnp.moveaxis(tiles, 0, dim).reshape(shape)


def gathered_copies(shard, axis, dim):
    tiles = copy_for_each(shard, axis)
    return laid_out(tiles, dim)


def in_blocks(shard, dim, devices):
    before, after = (shard.shape[:dim], shard.shape[dim + 1 :])
    return jnp.moveaxis(shard.reshape(*before, devices, -1, *after), dim, 0)


def summed_on_arrival(shard, axis, dim):
    tiles = in_blocks(shard, dim, lax.axis_size(axis))
    arrived = lax.all_to_all(tiles, axis, split_axis=0, concat_axis=0, tiled=True)
    return arrived.astype(jnp.float32).sum(axis=0)


def side_by_side(arrays, axis, dim, along):
    widths = [a.shape[along] for a in arrays]
    both = jnp.concatenate(arrays, axis=along)
    whole = lax.all_gather(both, axis, axis=dim, tiled=True)
    return tuple(jnp.split(whole, [sum(widths[:k]) for k in range(1, len(widths))], axis=along))


def sum_by_chip_2(shard, chips, core, dim):
    sizes = (lax.axis_size(chips), lax.axis_size(core))
    tiles = in_blocks(shard, dim, sizes[0] * sizes[1])
    inside = tiles.shape[1:]
    tiles = tiles.reshape(*sizes, *inside).swapaxes(0, 1).reshape(-1, *inside)
    tiles = lax.psum_scatter(tiles, core, scatter_dimension=0, tiled=True)
    return lax.psum_scatter(tiles, chips, scatter_dimension=0, tiled=True)[0]


def normalize(values):
    center = values - jnp.mean(values, axis=-1, keepdims=True)
    spread = jnp.mean(center * center, axis=-1, keepdims=True)
    return center * lax.rsqrt(spread + 1e-06)


def per_device(
    tokens, norm_gain, w_query, w_key, w_value, w_inner, bias_inner, w_attn_out, w_outer, temper
):
    local = tokens.astype(jnp.float32)
    normed = (normalize(local) * norm_gain).astype(jnp.bfloat16)
    image = gathered_copies(normed, MP, 0)
    count_rows = image.shape[0]
    width_head = w_query.shape[1]
    spread_rows = lax.all_to_all(image, "dp", split_axis=1, concat_axis=0, tiled=True)
    stacked = jnp.concatenate((w_query, w_key, w_value, w_inner), axis=1)
    projected = summed_on_arrival(
        jnp.dot(spread_rows, stacked, preferred_element_type=jnp.float32).astype(jnp.bfloat16),
        "dp",
        0,
    )
    query_sum = projected[:, :width_head]
    key_sum = projected[:, width_head : 2 * width_head]
    value_sum = projected[:, 2 * width_head : 3 * width_head]
    inner_sum = projected[:, 3 * width_head :]
    heads_dev = width_head // HEAD
    shape = (count_rows, heads_dev, HEAD)
    query_norm = normalize(
        query_sum.astype(jnp.bfloat16).astype(jnp.float32).reshape(shape)
    ).astype(jnp.bfloat16)
    key_norm = normalize(key_sum.astype(jnp.bfloat16).astype(jnp.float32).reshape(shape)).astype(
        jnp.bfloat16
    )
    values = value_sum.astype(jnp.bfloat16).reshape(shape)
    scale = temper / math.sqrt(HEAD)
    scores = jnp.einsum("qhc,khc->hqk", query_norm, key_norm, preferred_element_type=jnp.float32)
    scores = scores * scale[:, None, None]
    probs = jax.nn.softmax(scores, axis=-1).astype(jnp.bfloat16)
    mixed = jnp.einsum("hqk,khc->qhc", probs, values, preferred_element_type=jnp.float32)
    mixed = mixed.astype(jnp.bfloat16).reshape(count_rows, width_head)
    inner = inner_sum + bias_inner
    activ = jax.nn.gelu(inner, approximate=False).astype(jnp.bfloat16)
    attn_full, outer_full = side_by_side((w_attn_out, w_outer), "dp", 1, 0)
    total = sum_by_chip_2(
        (
            jnp.dot(mixed, attn_full, preferred_element_type=jnp.float32)
            + jnp.dot(activ, outer_full, preferred_element_type=jnp.float32)
        ).astype(jnp.bfloat16),
        ("mp_0", "mp_1"),
        "mp_2",
        0,
    ).astype(jnp.float32)
    return (local + total).astype(jnp.bfloat16)


def solution(mesh):
    finer = Mesh(mesh.devices.reshape(mesh.shape["dp"], 8, 2, 2), ("dp", "mp_0", "mp_1", "mp_2"))
    return jax.shard_map(
        per_device,
        mesh=finer,
        in_specs=(
            P(DP_MP, None),
            P(),
            P("dp", MP),
            P("dp", MP),
            P("dp", MP),
            P("dp", MP),
            P(MP),
            P(MP, "dp"),
            P(MP, "dp"),
            P(MP),
        ),
        out_specs=P(DP_MP, None),
        check_vma=False,
    )
```

profile of v0, /device:TPU:8, one launch (start us, length us, event | category | flops | bytes accessed | tf_op | source)
XLA Modules:
  0.0 410.7 jit_solution(5217342773899840325)
XLA Ops:
  6.5 2.5 pad_maximum_fusion
  9.2 0.2 fusion.56
  9.6 0.7 broadcast_in_dim.2
  10.3 51.8 %all_to_all.29 = bf16[32,4,6144]{2,1,0:T(4,128)(2,1)S(1)} all-to-all(bf16[32,4,6144]{2,1,0:T(4,128)(2,1)S(1)} %broadcast_in_dim.2), channel_id=1, replica_groups=mesh['dp'=8,'mp_0'=8,'mp_1'=2,'mp_2'=2] {'mp_0','mp_1','mp_2'}, dimensions={0} | all-to-all | bytes 3145728 | tf_op jit(solution)/shard_map/all_to_all | solution.py:16
  62.1 1.2 all_to_all.21
  63.3 0.3 copy.17
  63.6 40.8 %all_to_all.30 = bf16[128,8,768]{2,0,1:T(8,128)(2,1)S(1)} all-to-all(bf16[128,8,768]{2,0,1:T(8,128)(2,1)S(1)} %copy.17), channel_id=1, replica_groups=mesh['dp'=8,'mp_0'=8,'mp_1'=2,'mp_2'=2] {'dp'}, dimensions={1} | all-to-all | bytes 3145728 | tf_op jit(solution)/shard_map/all_to_all | solution.py:71
  104.5 3.7 convolution_convert_fusion
  108.2 5.8 %all-to-all-start.2 = ((bf16[8,128,1152]{2,1,0:T(8,128)(2,1)}), bf16[8,128,1152]{2,1,0:T(8,128)(2,1)S(1)}, u32[]{:S(2)}, u32[]{:S(2)}) async-start(bf16[8,128,1152]{2,1,0:T(8,128)(2,1)} %bitcast.23), calls=%async_computation.2 | async-start | bytes 4718592 | tf_op jit(solution)/shard_map/all_to_all | solution.py:37
  114.6 46.7 %all-to-all-done.2 = bf16[8,128,1152]{2,1,0:T(8,128)(2,1)S(1)} async-done(((bf16[8,128,1152]{2,1,0:T(8,128)(2,1)}), bf16[8,128,1152]{2,1,0:T(8,128)(2,1)S(1)}, u32[]{:S(2)}, u32[]{:S(2)}) %all-to-all-start.2) | async-done | bytes 2359328 | tf_op jit(solution)/shard_map/all_to_all | solution.py:37
  161.4 0.3 convert_reduce_fusion
  161.8 0.2 fusion.66
  162.0 0.3 fusion.114
  162.4 18.3 %all-gather.2.cloned.1.call-done = bf16[896,6144]{1,0:T(8,128)(2,1)} async-done(((bf16[896,768]{1,0:T(8,128)(2,1)}), bf16[896,6144]{1,0:T(8,128)(2,1)}) %all-gather.2.cloned.1.call-update) | async-done | bytes 11010064 | tf_op jit(solution)/shard_map/all_gather | solution.py:44
  180.6 7.6 %fusion = f32[128,6144]{1,0:T(8,128)} fusion(bf16[896,6144]{1,0:T(8,128)(2,1)} %all-gather.2.cloned.1.call-done, f32[128,1152]{1,0:T(8,128)S(1)} %convert_reduce_fusion, f32[768]{0:T(1024)S(1)} %copy-done.6), kind=kOutput, calls=%fused_computation | convolution fusion | flops 1214447616 | bytes 12980224 | tf_op jit(solution)/shard_map/dot_general | solution.py:103
  188.3 3.1 fusion.2
  191.4 0.6 reshape_reshape.3
  192.0 1.8 copy.18
  193.9 0.6 dynamic-slice
  195.2 42.8 %all-reduce.5.cloned.1.call-done = bf16[32,4,6144]{2,1,0:T(4,128)(2,1)} async-done(((bf16[32,4,6144]{2,1,0:T(4,128)(2,1)}), bf16[32,4,6144]{2,1,0:T(4,128)(2,1)}) %all-reduce.5.cloned.1.call-update) | async-done | bytes 1572880
  238.0 2.3 constant_dynamic-slice_fusion
  240.4 0.7 dynamic-slice.2
  241.0 161.0 %all-reduce.7.cloned.1.call-done = bf16[16,4,6144]{2,1,0:T(4,128)(2,1)} async-done(((bf16[16,4,6144]{2,1,0:T(4,128)(2,1)}), bf16[16,4,6144]{2,1,0:T(4,128)(2,1)}) %all-reduce.7.cloned.1.call-update) | async-done | bytes 786448
  402.1 2.1 fusion.59
  (34 shorter events, 0.6 us)
Async XLA Ops:
  6.5 2.5 copy-start
  6.5 2.9 copy-start.1
  6.5 174.1 %all-gather.2.cloned.1.call-start = ((), (), s32[]{:S(2)}) async-start(), calls=%async_computation.3 | async-start | bytes 12386304 | tf_op jit(solution)/shard_map/all_gather | solution.py:44
  63.6 40.9 %copy-start.2 = (bf16[768,768]{1,0:T(8,128)(2,1)S(1)}, bf16[768,768]{1,0:T(8,128)(2,1)}, u32[]{:S(2)}) copy-start(bf16[768,768]{1,0:T(8,128)(2,1)} %param.15) | copy-start | bytes 3538948
  63.6 40.9 %copy-start.3 = (bf16[768,128]{1,0:T(8,128)(2,1)S(1)}, bf16[768,128]{1,0:T(8,128)(2,1)}, u32[]{:S(2)}) copy-start(bf16[768,128]{1,0:T(8,128)(2,1)} %param.14) | copy-start | bytes 589828
  63.6 40.9 %copy-start.4 = (bf16[768,128]{1,0:T(8,128)(2,1)S(1)}, bf16[768,128]{1,0:T(8,128)(2,1)}, u32[]{:S(2)}) copy-start(bf16[768,128]{1,0:T(8,128)(2,1)} %param.13) | copy-start | bytes 589828
  63.6 40.9 %copy-start.5 = (bf16[768,128]{1,0:T(8,128)(2,1)S(1)}, bf16[768,128]{1,0:T(8,128)(2,1)}, u32[]{:S(2)}) copy-start(bf16[768,128]{1,0:T(8,128)(2,1)} %param.12) | copy-start | bytes 589828
  108.2 53.2 %all-to-all-start.2 = ((bf16[8,128,1152]{2,1,0:T(8,128)(2,1)}), bf16[8,128,1152]{2,1,0:T(8,128)(2,1)S(1)}, u32[]{:S(2)}, u32[]{:S(2)}) async-start(bf16[8,128,1152]{2,1,0:T(8,128)(2,1)} %bitcast.23), calls=%async_computation.2 | async-start | bytes 4718592 | tf_op jit(solution)/shard_map/all_to_all | solution.py:37
  113.9 124.1 %all-reduce.5.cloned.1.call-start = ((), (), s32[]{:S(2)}) async-start(), calls=%async_computation.4 | async-start | bytes 3145728
  114.6 66.0 %copy-start.6 = (f32[768]{0:T(1024)S(1)}, f32[768]{0:T(1024)}, u32[]{:S(2)}) copy-start(f32[768]{0:T(1024)} %param.16) | copy-start | bytes 9220
  192.0 1.9 copy-start.8
  193.9 46.5 %copy-start.7 = (u32[256]{0:T(256)S(1)}, u32[256]{0:T(256)}, u32[]{:S(2)}) copy-start(u32[256]{0:T(256)} %constant.88) | copy-start | bytes 3076
  193.9 208.2 %all-reduce.7.cloned.1.call-start = ((), (), s32[]{:S(2)}) async-start(), calls=%async_computation.5 | async-start | bytes 1572864
Sparse Core Ops, SparseCore 0:
  9.2 171.4 all-gather.1
  194.0 43.9 all-reduce.4
  240.6 161.3 all-reduce.6
where the time goes:
time: 411 us
  waiting for transfers between devices  269 us (65%)
  blocking collectives  92.6 us (23%)
  matrix products  14.7 us (4%)
  between operations  14.6 us (4%)
  local copies, waits for them, and re-layouts  8.21 us (2%)
  starting transfers between devices  5.83 us (1%)
  other arithmetic  5.76 us (1%)
    unnamed x5, waiting for transfers between devices  204 us
    all_to_all x1, blocking collectives, copy_for_each(): return lax.all_to_all(copies, axis, split_axis=0, concat_axis=0, tiled=True)  51.8 us
    all_to_all x1, waiting for transfers between devices, summed_on_arrival(): lax.all_to_all(tiles, axis, split_axis=0, concat_axis=0, tiled=True)  46.7 us
    all_to_all x1, blocking collectives, per_device(): lax.all_to_all(image, 'dp', split_axis=1, concat_axis=0, tiled=True)  40.8 us
    all_gather x1, waiting for transfers between devices, side_by_side(): whole = lax.all_gather(both, axis, axis=dim, tiled=True)  18.3 us
  transfers between devices with their start and end apart: 4, of which 4 were waited for; matrix products, arithmetic and copies ran while one was open for 2% of the time, Pallas kernels for 0%

commit v1 on v0

v1 whole, which is shorter than its diff:
```python
import math

import jax
import jax.numpy as jnp
from jax import lax
from jax.experimental import pallas as pl
from jax.experimental.pallas import tpu as pltpu
from jax.sharding import PartitionSpec as P

HEAD = 128
IMAGES = 8
PLANES = 8
ROWS = 4
WIDTH = 768
BLOCK = 128
STRIP = 16
HIDDEN = 768
FIRST = 3 * HEAD + HIDDEN
SECOND = HEAD + HIDDEN
OFFSETS = (1, -1, 2, -2, 3, -3, 4)
MESH = pl.DeviceIdType.MESH
F32 = jnp.float32
BF16 = jnp.bfloat16


def offset_of(step):
    return ((step + 1) // 2) * (2 * (step % 2) - 1)


def normalize(values):
    center = values - jnp.mean(values, axis=-1, keepdims=True)
    spread = jnp.mean(center * center, axis=-1, keepdims=True)
    return center * lax.rsqrt(spread + 1e-06)


def gathered_row(place):
    image, within = place >> 4, place & 15
    return ((within >> 2) & 1) * 64 + (within >> 3) * 32 + image * 4 + (within & 3)


def to_strips():
    row = lax.broadcasted_iota(jnp.int32, (BLOCK, BLOCK), 0)
    column = lax.broadcasted_iota(jnp.int32, (BLOCK, BLOCK), 1)
    return jnp.where(column == gathered_row(row), 1.0, 0.0).astype(BF16)


def from_strips():
    row = lax.broadcasted_iota(jnp.int32, (BLOCK, BLOCK), 0)
    column = lax.broadcasted_iota(jnp.int32, (BLOCK, BLOCK), 1)
    return jnp.where(row == gathered_row(column), 1.0, 0.0).astype(BF16)


def kernel(
    tokens,
    gain,
    w_query,
    w_key,
    w_value,
    w_inner,
    bias,
    w_attn_out,
    w_outer,
    temper,
    out,
    first,
    second,
    norm_out,
    norm_in,
    lines,
    planes,
    part_out,
    part_in,
    strips,
    acts,
    pair_own,
    pair_out,
    pair_in,
    plane_out,
    plane_in,
    cross_out,
    cross_in,
    final_out,
    final_in,
    w_sem,
    norm_sem,
    x_sem,
    z_sem,
    core_sem,
    part_sem,
    acts_sem,
    pair_sem,
    plane_sem,
    cross_sem,
    final_sem,
):
    dp = lax.axis_index("dp")
    mp = lax.axis_index("mp")
    z, lane = mp // 4, mp % 4
    x_hi, core = lane // 2, lane % 2
    other_core = (dp, mp + 1 - 2 * core)
    other_x = (dp, mp + 2 - 4 * x_hi)

    def plane_device(plane):
        return (dp, plane * 4 + lane)

    def around(offset):
        return lax.rem(z + offset + PLANES, PLANES)

    def image_at(step):
        return lax.rem(dp + step, IMAGES)

    def image_before(step):
        return lax.rem(dp - step + IMAGES, IMAGES)

    def send(source, target, sems, index, device):
        return pltpu.make_async_remote_copy(
            src_ref=source,
            dst_ref=target,
            send_sem=sems.at[(0, *index)],
            recv_sem=sems.at[(1, *index)],
            device_id=device,
            device_id_type=MESH,
        )

    weights = [
        pltpu.make_async_copy(w_query, first.at[:, pl.ds(0, HEAD)], w_sem.at[0]),
        pltpu.make_async_copy(w_key, first.at[:, pl.ds(HEAD, HEAD)], w_sem.at[1]),
        pltpu.make_async_copy(w_value, first.at[:, pl.ds(2 * HEAD, HEAD)], w_sem.at[2]),
        pltpu.make_async_copy(w_inner, first.at[:, pl.ds(3 * HEAD, HIDDEN)], w_sem.at[3]),
        pltpu.make_async_copy(w_attn_out, second.at[pl.ds(0, HEAD), :], w_sem.at[4]),
        pltpu.make_async_copy(w_outer, second.at[pl.ds(HEAD, HIDDEN), :], w_sem.at[5]),
    ]
    barrier = pltpu.get_barrier_semaphore()
    peers = [(image_at(step), mp) for step in range(1, IMAGES)]
    peers += [plane_device(around(offset)) for offset in OFFSETS]
    peers += [other_core, other_x]
    for peer in peers:
        pl.semaphore_signal(barrier, inc=1, device_id=peer, device_id_type=MESH)
    for copy in weights:
        copy.start()

    normed = (normalize(tokens[...].astype(F32)) * gain[...]).astype(BF16)
    for block in range(IMAGES):
        norm_out[block] = normed[:, block * WIDTH : (block + 1) * WIDTH]
    pl.semaphore_wait(barrier, len(peers))

    def norm_copy(step):
        return send(norm_out.at[image_at(step)], norm_in.at[dp], norm_sem, (step,), (image_at(step), mp))

    def norm_landed(step):
        place = norm_in.at[image_before(step)]
        return send(place, place, norm_sem, (step,), (image_before(step), mp))

    for step in range(1, IMAGES):
        norm_copy(step).start()
    norm_in[dp] = norm_out[dp]
    for step in range(1, IMAGES):
        norm_landed(step).wait_recv()
    for image in range(IMAGES):
        lines[pl.ds(image * ROWS, ROWS), :] = norm_in[image].astype(F32)
    planes[z, core, x_hi] = lines[...].astype(BF16)

    def x_copy(side):
        place = planes.at[z, core, side]
        return send(place, place, x_sem, (), other_x)

    def z_copy(side, step):
        place = planes.at[z, core, side]
        return send(place, place, z_sem, (side, step), plane_device(around(OFFSETS[step])))

    def z_landed(side, step, plane):
        place = planes.at[plane, core, side]
        return send(place, place, z_sem, (side, step), plane_device(plane))

    def core_copy(plane, side):
        place = planes.at[plane, side]
        return send(place, place, core_sem, (plane,), other_core)

    x_copy(x_hi).start()
    for step in range(len(OFFSETS)):
        z_copy(x_hi, step).start()
    x_copy(1 - x_hi).wait_recv()
    for step in range(len(OFFSETS)):
        z_copy(1 - x_hi, step).start()
    core_copy(z, core).start()
    for copy in weights[:4]:
        copy.wait()

    def part_copy(plane, step):
        image = image_at(step)
        return send(part_out.at[plane, image], part_in.at[plane, dp], part_sem, (plane, step), (image, mp))

    def part_landed(plane, step):
        image = image_before(step)
        place = part_in.at[plane, image]
        return send(place, place, part_sem, (plane, step), (image, mp))

    def project(step, carry):
        @pl.when(step + 1 < PLANES)
        def _():
            plane = around(-offset_of(step + 1))
            z_landed(x_hi, step, plane).wait_recv()
            z_landed(1 - x_hi, step, plane).wait_recv()
            core_copy(plane, core).start()

        plane = around(-offset_of(step))
        core_copy(plane, 1 - core).wait_recv()
        rows = jnp.dot(
            to_strips(), planes[plane].reshape(BLOCK, WIDTH), preferred_element_type=F32
        ).astype(BF16)
        part = jnp.dot(rows, first[...], preferred_element_type=F32).astype(BF16)
        part_out[plane] = part.reshape(IMAGES, STRIP, FIRST)

        def go(ahead, carry):
            part_copy(plane, ahead).start()
            return carry

        return lax.fori_loop(1, IMAGES, go, carry)

    lax.fori_loop(0, PLANES, project, 0)

    def collect(step, carry):
        plane = around(-offset_of(step))

        def landed(ahead, carry):
            part_landed(plane, ahead).wait_recv()
            return carry

        lax.fori_loop(1, IMAGES, landed, 0)
        part_in[plane, dp] = part_out[plane, dp]
        total = part_in[plane, 0].astype(F32)
        for image in range(1, IMAGES):
            total += part_in[plane, image].astype(F32)
        strips[plane] = total[:, : 3 * HEAD].astype(BF16).astype(F32)
        inner = total[:, 3 * HEAD :] + bias[...]
        activ = 0.5 * inner * (1.0 + lax.erf(inner * math.sqrt(0.5)))
        acts[plane, dp, :, HEAD:] = activ.astype(BF16)
        return carry

    lax.fori_loop(0, PLANES, collect, 0)

    whole = strips[...].reshape(BLOCK, 3 * HEAD)
    query_norm = normalize(whole[:, :HEAD]).astype(BF16)
    key_norm = normalize(whole[:, HEAD : 2 * HEAD]).astype(BF16)
    scores = lax.dot_general(
        query_norm, key_norm, (((1,), (1,)), ((), ())), preferred_element_type=F32
    ) * (temper[...] / math.sqrt(HEAD))
    weight = jnp.exp(scores - jnp.max(scores, axis=-1, keepdims=True))
    probs = (weight / jnp.sum(weight, axis=-1, keepdims=True)).astype(BF16)
    mixed = jnp.dot(probs, whole[:, 2 * HEAD :].astype(BF16), preferred_element_type=F32)
    mixed = mixed.astype(BF16).reshape(PLANES, STRIP, HEAD)
    for plane in range(PLANES):
        acts[plane, dp, :, :HEAD] = mixed[plane]

    def acts_copy(plane, step):
        place = acts.at[plane, dp]
        return send(place, place, acts_sem, (plane, step), (image_at(step), mp))

    def acts_landed(plane, step):
        image = image_before(step)
        place = acts.at[plane, image]
        return send(place, place, acts_sem, (plane, step), (image, mp))

    def spread(step, carry):
        plane = around(offset_of(PLANES - 1 - step))

        def go(ahead, carry):
            acts_copy(plane, ahead).start()
            return carry

        return lax.fori_loop(1, IMAGES, go, carry)

    lax.fori_loop(0, PLANES, spread, 0)
    for copy in weights[4:]:
        copy.wait()

    def pair_copy(plane):
        return send(pair_out.at[plane], pair_in.at[plane], pair_sem, (plane,), other_core)

    def plane_copy(plane, slot):
        return send(plane_out.at[plane], plane_in.at[slot], plane_sem, (slot,), plane_device(plane))

    def plane_landed(slot):
        place = plane_in.at[slot]
        return send(place, place, plane_sem, (slot,), plane_device(around(-offset_of(slot + 1))))

    def pass_on(slot, plane):
        pair_copy(plane).wait_recv()
        total = pair_own[plane] + pair_in[plane].astype(F32)
        pair_own[plane] = total
        plane_out[plane] = total.astype(BF16)

    def output(step, carry):
        @pl.when(step < PLANES)
        def _():
            plane = around(offset_of(PLANES - 1 - step))

            def landed(ahead, carry):
                acts_landed(plane, ahead).wait_recv()
                return carry

            lax.fori_loop(1, IMAGES, landed, 0)
            rows = jnp.dot(
                from_strips(), acts[plane].reshape(BLOCK, SECOND), preferred_element_type=F32
            ).astype(BF16)
            part = jnp.dot(rows, second[...], preferred_element_type=F32).reshape(2, 64, WIDTH)
            low, high = part[0], part[1]
            pair_own[plane] = jnp.where(core == 0, low, high)
            pair_out[plane] = jnp.where(core == 0, high, low).astype(BF16)
            pair_copy(plane).start()

        @pl.when(step >= 1)
        def _():
            slot = PLANES - 1 - step
            plane = around(offset_of(slot + 1))
            pass_on(slot, plane)

            @pl.when(step < PLANES)
            def _():
                plane_copy(plane, slot).start()

        return carry

    lax.fori_loop(0, PLANES + 1, output, 0)
    total = pair_own[z]
    for slot in reversed(range(PLANES - 1)):
        plane_landed(slot).wait_recv()
        total += plane_in[slot].astype(F32)
    sides = total.reshape(2, 32, WIDTH)
    mine = jnp.where(x_hi == 0, sides[0], sides[1])
    cross_out[...] = jnp.where(x_hi == 0, sides[1], sides[0]).astype(BF16)
    cross = send(cross_out, cross_in, cross_sem, (), other_x)
    cross.start()
    cross.wait_recv()
    lines[...] = mine + cross_in[...].astype(F32)
    for image in range(IMAGES):
        final_out[image] = lines[pl.ds(image * ROWS, ROWS), :].astype(BF16)

    def final_copy(step):
        return send(final_out.at[image_at(step)], final_in.at[dp], final_sem, (step,), (image_at(step), mp))

    def final_landed(step):
        place = final_in.at[image_before(step)]
        return send(place, place, final_sem, (step,), (image_before(step), mp))

    for step in range(1, IMAGES):
        final_copy(step).start()
    final_in[dp] = final_out[dp]
    for step in range(1, IMAGES):
        final_landed(step).wait_recv()
    for block in range(IMAGES):
        columns = pl.ds(block * WIDTH, WIDTH)
        out[:, columns] = (tokens[:, columns].astype(F32) + final_in[block].astype(F32)).astype(BF16)

    for step in range(1, IMAGES):
        norm_copy(step).wait_send()
        final_copy(step).wait_send()
    x_copy(x_hi).wait_send()
    cross.wait_send()
    for step in range(len(OFFSETS)):
        z_copy(x_hi, step).wait_send()
        z_copy(1 - x_hi, step).wait_send()

    def sent(plane, carry):
        core_copy(plane, core).wait_send()
        pair_copy(plane).wait_send()

        def one(ahead, carry):
            part_copy(plane, ahead).wait_send()
            acts_copy(plane, ahead).wait_send()
            return carry

        return lax.fori_loop(1, IMAGES, one, carry)

    lax.fori_loop(0, PLANES, sent, 0)
    for slot in range(PLANES - 1):
        plane_copy(around(offset_of(slot + 1)), slot).wait_send()


def per_device(
    tokens, norm_gain, w_query, w_key, w_value, w_inner, bias_inner, w_attn_out, w_outer, temper
):
    vmem = pl.BlockSpec(memory_space=pltpu.VMEM)
    anywhere = pl.BlockSpec(memory_space=pl.ANY)
    dma = pltpu.SemaphoreType.DMA
    return pl.pallas_call(
        kernel,
        out_shape=jax.ShapeDtypeStruct(tokens.shape, BF16),
        in_specs=[vmem, vmem, anywhere, anywhere, anywhere, anywhere, vmem, anywhere, anywhere, vmem],
        out_specs=vmem,
        scratch_shapes=[
            pltpu.VMEM((WIDTH, FIRST), BF16),
            pltpu.VMEM((SECOND, WIDTH), BF16),
            pltpu.VMEM((IMAGES, ROWS, WIDTH), BF16),
            pltpu.VMEM((IMAGES, ROWS, WIDTH), BF16),
            pltpu.VMEM((32, WIDTH), F32),
            pltpu.VMEM((PLANES, 2, 2, 32, WIDTH), BF16),
            pltpu.VMEM((PLANES, IMAGES, STRIP, FIRST), BF16),
            pltpu.VMEM((PLANES, IMAGES, STRIP, FIRST), BF16),
            pltpu.VMEM((PLANES, STRIP, 3 * HEAD), F32),
            pltpu.VMEM((PLANES, IMAGES, STRIP, SECOND), BF16),
            pltpu.VMEM((PLANES, 64, WIDTH), F32),
            pltpu.VMEM((PLANES, 64, WIDTH), BF16),
            pltpu.VMEM((PLANES, 64, WIDTH), BF16),
            pltpu.VMEM((PLANES, 64, WIDTH), BF16),
            pltpu.VMEM((PLANES - 1, 64, WIDTH), BF16),
            pltpu.VMEM((32, WIDTH), BF16),
            pltpu.VMEM((32, WIDTH), BF16),
            pltpu.VMEM((IMAGES, ROWS, WIDTH), BF16),
            pltpu.VMEM((IMAGES, ROWS, WIDTH), BF16),
            dma((6,)),
            dma((2, IMAGES)),
            dma((2,)),
            dma((2, 2, PLANES - 1)),
            dma((2, PLANES)),
            dma((2, PLANES, IMAGES)),
            dma((2, PLANES, IMAGES)),
            dma((2, PLANES)),
            dma((2, PLANES - 1)),
            dma((2,)),
            dma((2, IMAGES)),
        ],
        compiler_params=pltpu.CompilerParams(
            collective_id=0, has_side_effects=True, vmem_limit_bytes=48 * 1024 * 1024
        ),
    )(
        tokens,
        norm_gain.reshape(1, -1),
        w_query,
        w_key,
        w_value,
        w_inner,
        bias_inner.reshape(1, -1),
        w_attn_out,
        w_outer,
        temper.reshape(1, 1),
    )


def solution(mesh):
    return jax.shard_map(
        per_device,
        mesh=mesh,
        in_specs=(
            P(("dp", "mp"), None),
            P(),
            P("dp", "mp"),
            P("dp", "mp"),
            P("dp", "mp"),
            P("dp", "mp"),
            P("mp"),
            P("mp", "dp"),
            P("mp", "dp"),
            P("mp"),
        ),
        out_specs=P(("dp", "mp"), None),
        check_vma=False,
    )
```

time: 411 us -> 104 us (0.25)
  waiting for transfers between devices: 269 us -> 0 us
  Pallas kernels: 0 us -> 93.5 us
  blocking collectives: 92.6 us -> 0 us
  matrix products: 14.7 us -> 0 us
  between operations: 14.6 us -> 0.67 us
  starting transfers between devices: 5.83 us -> 0 us
  other arithmetic: 5.76 us -> 0 us
    unnamed x5 -> x0, waiting for transfers between devices: 204 us -> none
    pallas_call x0 -> x1, Pallas kernels: none -> 93.5 us  [per_device(): pl.pallas_call(kernel, out_shape=jax.ShapeDtypeStruct(tokens.shape, BF16)...]
    all_to_all x2 -> x0, blocking collectives: 92.6 us -> none  [the longest x1 51.8 us: copy_for_each(): return lax.all_to_all(copies, axis, split_axis=0, concat_axis=0, tiled=True)]
    all_to_all x1 -> x0, waiting for transfers between devices: 46.7 us -> none  [summed_on_arrival(): lax.all_to_all(tiles, axis, split_axis=0, concat_axis=0, tiled=True)]
    all_gather x1 -> x0, waiting for transfers between devices: 18.3 us -> none  [side_by_side(): whole = lax.all_gather(both, axis, axis=dim, tiled=True)]
    dot_general x4 -> x0, matrix products: 14.7 us -> none  [the longest x1 7.62 us: per_device(): jnp.dot(activ, outer_full, preferred_element_type=jnp.float32)]
    all_to_all x1 -> x0, starting transfers between devices: 5.78 us -> none  [summed_on_arrival(): lax.all_to_all(tiles, axis, split_axis=0, concat_axis=0, tiled=True)]
    unnamed x21 -> x17, local copies, waits for them, and re-layouts: 3.6 us -> 8.4 us
  transfers between devices with their start and end apart: 4 -> 0, of which waited for: 4 -> 0; matrix products, arithmetic and copies ran while one was open for 2% -> 0% of each run, Pallas kernels for 0% -> 0%
where the time goes in v1:
time: 104 us; the launch traced here: 103 us
  Pallas kernels  93.5 us (90%)
  local copies, waits for them, and re-layouts  9.09 us (9%)
    pallas_call x1, Pallas kernels, per_device(): pl.pallas_call(kernel, out_shape=jax.ShapeDtypeStruct(tokens.shape, BF16)...  93.5 us
    unnamed x17, local copies, waits for them, and re-layouts  8.4 us

profile of v1, /device:TPU:8, one launch (start us, length us, event | category | flops | bytes accessed | tf_op | source)
XLA Modules:
  0.0 103.3 jit_solution(6318556813368699921)
XLA Ops:
  0.7 0.7 reshape.10.bias
  1.3 0.0 copy-start
  1.3 1.3 %copy-done = bf16[768,768]{1,0:T(8,128)(2,1)S(1)} copy-done((bf16[768,768]{1,0:T(8,128)(2,1)S(1)}, bf16[768,768]{1,0:T(8,128)(2,1)}, u32[]{:S(2)}) %copy-start) | copy-done | bytes 1179672
  2.6 0.0 copy-start.1
  2.6 1.3 %copy-done.1 = bf16[768,768]{1,0:T(8,128)(2,1)S(1)} copy-done((bf16[768,768]{1,0:T(8,128)(2,1)S(1)}, bf16[768,768]{1,0:T(8,128)(2,1)}, u32[]{:S(2)}) %copy-start.1) | copy-done | bytes 1179672
  3.9 0.0 copy-start.2
  3.9 0.9 copy-done.2
  4.8 0.0 copy-start.3
  4.8 0.9 copy-done.3
  5.7 0.0 copy-start.4
  5.7 0.9 copy-done.4
  6.7 0.0 copy-start.5
  6.7 0.9 copy-done.5
  7.6 0.0 copy-start.6
  7.6 0.8 copy-done.6
  8.4 0.0 copy-start.7
  8.4 0.7 copy-done.7
  9.1 93.5 %shard_map.100 = bf16[4,6144]{1,0:T(4,128)(2,1)S(1)} custom-call(bf16[4,6144]{1,0:T(4,128)(2,1)S(1)} %copy-done.6, f32[1,6144]{1,0:T(1,128)S(1)} %bitcast.3, bf16[768,128]{1,0:T(8,128)(2,1)S(1)} %copy-done.2, bf16[768,128]{1,0:T(8,128)(2,1)S(1)} %copy-done.3, bf16[768,128]{1,0:T(8,128)(2,1)S(1)} %copy-done.4, bf16[768,768]{1,0:T(8,128)(2,1)S(1)} %copy-done, ...), custom_call_target="tpu_custom_call" | custom-call | tf_op jit(solution)/shard_map/pallas_call | solution.py:386
  102.7 0.6 copy.13
Async XLA Ops:
  1.3 1.3 %copy-start = (bf16[768,768]{1,0:T(8,128)(2,1)S(1)}, bf16[768,768]{1,0:T(8,128)(2,1)}, u32[]{:S(2)}) copy-start(bf16[768,768]{1,0:T(8,128)(2,1)} %w_inner.1) | copy-start | bytes 3538948
  2.6 1.3 %copy-start.1 = (bf16[768,768]{1,0:T(8,128)(2,1)S(1)}, bf16[768,768]{1,0:T(8,128)(2,1)}, u32[]{:S(2)}) copy-start(bf16[768,768]{1,0:T(8,128)(2,1)} %w_outer.1) | copy-start | bytes 3538948
  3.9 0.9 copy-start.2
  4.8 0.9 copy-start.3
  5.7 0.9 copy-start.4
  6.7 0.9 copy-start.5
  7.6 0.8 copy-start.6
  8.4 0.7 copy-start.7

commit v2 on v1

v2 whole, which is shorter than its diff:
```python
import math

import jax
import jax.numpy as jnp
from jax import lax
from jax.experimental import pallas as pl
from jax.experimental.pallas import tpu as pltpu
from jax.sharding import PartitionSpec as P

HEAD = 128
IMAGES = 8
STACK = 4
PLANES = 8
ROWS = 4
WIDTH = 768
BLOCK = 128
STRIP = 16
HIDDEN = 768
FIRST = 3 * HEAD + HIDDEN
X_FIRST = 640
Y_FIRST = FIRST - X_FIRST
SECOND = HEAD + HIDDEN
LAG = 2
X_ACTS = 512
MESH = pl.DeviceIdType.MESH
F32 = jnp.float32
BF16 = jnp.bfloat16


def offset_of(step):
    return ((step + 1) // 2) * (2 * (step % 2) - 1)


def normalize(values):
    center = values - jnp.mean(values, axis=-1, keepdims=True)
    spread = jnp.mean(center * center, axis=-1, keepdims=True)
    return center * lax.rsqrt(spread + 1e-06)


def gathered_row(place):
    image, within = place >> 4, place & 15
    return ((within >> 2) & 1) * 64 + (within >> 3) * 32 + image * 4 + (within & 3)


def to_strips():
    row = lax.broadcasted_iota(jnp.int32, (BLOCK, BLOCK), 0)
    column = lax.broadcasted_iota(jnp.int32, (BLOCK, BLOCK), 1)
    return jnp.where(column == gathered_row(row), 1.0, 0.0).astype(BF16)


def from_strips():
    row = lax.broadcasted_iota(jnp.int32, (BLOCK, BLOCK), 0)
    column = lax.broadcasted_iota(jnp.int32, (BLOCK, BLOCK), 1)
    return jnp.where(row == gathered_row(column), 1.0, 0.0).astype(BF16)


def kernel(
    tokens_hbm,
    gain_hbm,
    w_query,
    w_key,
    w_value,
    w_inner,
    bias_hbm,
    w_attn_out,
    w_outer,
    temper,
    out,
    tokens,
    gain,
    bias,
    first,
    second,
    norm_out,
    norm_in,
    lines,
    planes,
    part,
    part_x,
    mid_x,
    fin_x,
    part_y,
    mid_y,
    keep_y,
    fin_y,
    strips,
    acts,
    pair_own,
    pair_out,
    pair_in,
    plane_out,
    plane_in,
    final_out,
    final_in,
    w_sem,
    norm_sem,
    z_sem,
    core_sem,
    part_sem,
    acts_sem,
    pair_sem,
    plane_sem,
    final_sem,
):
    dp = lax.axis_index("dp")
    mp = lax.axis_index("mp")
    z, lane = mp // 4, mp % 4
    x_hi, core = lane // 2, lane % 2
    x_lo, y = dp // STACK, dp % STACK
    other_core = (dp, mp + 1 - 2 * core)
    other_x_lo = ((1 - x_lo) * STACK + y, mp)

    def plane_device(plane):
        return (dp, plane * 4 + lane)

    def around(offset):
        return lax.rem(z + offset + PLANES, PLANES)

    def image_at(step):
        return lax.rem(dp + step, IMAGES)

    def image_before(step):
        return lax.rem(dp - step + IMAGES, IMAGES)

    def y_at(step):
        return lax.rem(y + step, STACK)

    def y_before(step):
        return lax.rem(y - step + STACK, STACK)

    def y_device(row):
        return (x_lo * STACK + row, mp)

    def send(source, target, sems, index, device):
        return pltpu.make_async_remote_copy(
            src_ref=source,
            dst_ref=target,
            send_sem=sems.at[(0, *index)],
            recv_sem=sems.at[(1, *index)],
            device_id=device,
            device_id_type=MESH,
        )

    weights = [
        pltpu.make_async_copy(tokens_hbm, tokens, w_sem.at[6]),
        pltpu.make_async_copy(gain_hbm, gain, w_sem.at[7]),
        pltpu.make_async_copy(w_query, first.at[:, pl.ds(0, HEAD)], w_sem.at[0]),
        pltpu.make_async_copy(w_key, first.at[:, pl.ds(HEAD, HEAD)], w_sem.at[1]),
        pltpu.make_async_copy(w_value, first.at[:, pl.ds(2 * HEAD, HEAD)], w_sem.at[2]),
        pltpu.make_async_copy(w_inner, first.at[:, pl.ds(3 * HEAD, HIDDEN)], w_sem.at[3]),
        pltpu.make_async_copy(bias_hbm, bias, w_sem.at[8]),
        pltpu.make_async_copy(w_attn_out, second.at[pl.ds(0, HEAD), :], w_sem.at[4]),
        pltpu.make_async_copy(w_outer, second.at[pl.ds(HEAD, HIDDEN), :], w_sem.at[5]),
    ]
    for copy in weights[:2]:
        copy.start()
    pieces = [(step, flip) for step in range(IMAGES) for flip in range(2) if step or flip]

    def half(flip):
        return (1 - x_hi) if flip else x_hi

    def half_mp(flip):
        return z * 4 + half(flip) * 2 + core

    barrier = pltpu.get_barrier_semaphore()
    peers = [plane_device(around(offset_of(step))) for step in reversed(range(1, PLANES))]
    peers += [(image_at(step), half_mp(flip)) for step, flip in pieces] + [other_core]
    for peer in peers:
        pl.semaphore_signal(barrier, inc=1, device_id=peer, device_id_type=MESH)
    for copy in weights[2:]:
        copy.start()
    for copy in weights[:2]:
        copy.wait()

    normed = (normalize(tokens[...].astype(F32)) * gain[...]).astype(BF16)
    for block in range(IMAGES):
        norm_out[block] = normed[:, block * WIDTH : (block + 1) * WIDTH]
    pl.semaphore_wait(barrier, len(peers))

    def norm_copy(step, flip):
        return send(
            norm_out.at[image_at(step)],
            norm_in.at[dp, x_hi],
            norm_sem,
            (step, flip),
            (image_at(step), half_mp(flip)),
        )

    def norm_landed(step, flip):
        place = norm_in.at[image_before(step), half(flip)]
        return send(place, place, norm_sem, (step, flip), (image_before(step), half_mp(flip)))

    for piece in pieces:
        norm_copy(*piece).start()
    norm_in[dp, x_hi] = norm_out[dp]
    for piece in pieces:
        norm_landed(*piece).wait_recv()
    for side in range(2):
        for image in range(IMAGES):
            lines[pl.ds(side * 32 + image * ROWS, ROWS), :] = norm_in[image, side].astype(F32)
    planes[z, core] = lines[...].astype(BF16)

    def z_copy(step):
        place = planes.at[z, core]
        return send(place, place, z_sem, (step,), plane_device(around(offset_of(step))))

    def z_landed(step):
        plane = around(-offset_of(step))
        place = planes.at[plane, core]
        return send(place, place, z_sem, (step,), plane_device(plane))

    def core_copy(plane, side):
        place = planes.at[plane, side]
        return send(place, place, core_sem, (plane,), other_core)

    core_copy(z, core).start()
    for step in range(1, PLANES):
        z_copy(step).start()
    for copy in weights[2:6]:
        copy.wait()

    left, right = pl.ds(0, X_FIRST), pl.ds(X_FIRST, Y_FIRST)

    def part_x_copy(plane):
        return send(
            part.at[plane, 1 - x_lo, :, :, left], part_x.at[plane], part_sem, (plane, 0), other_x_lo
        )

    def part_y_copy(plane, step):
        return send(
            part.at[plane, :, y_at(step), :, right],
            part_y.at[plane, step - 1],
            part_sem,
            (plane, step),
            y_device(y_at(step)),
        )

    def mid_x_copy(plane, step):
        return send(
            mid_x.at[plane, y_at(step)],
            fin_x.at[plane, step - 1],
            part_sem,
            (plane, 3 + step),
            y_device(y_at(step)),
        )

    def mid_y_copy(plane):
        return send(mid_y.at[plane], fin_y.at[plane], part_sem, (plane, 7), other_x_lo)

    def project(step):
        plane = around(-offset_of(step))
        core_copy(plane, 1 - core).wait_recv()
        rows = jnp.dot(
            to_strips(), planes[plane].reshape(BLOCK, WIDTH), preferred_element_type=F32
        ).astype(BF16)
        for columns, width in ((left, X_FIRST), (right, Y_FIRST)):
            block = jnp.dot(rows, first[:, columns], preferred_element_type=F32)
            part[plane, :, :, :, columns] = block.astype(BF16).reshape(2, STACK, STRIP, width)
        part_x_copy(plane).start()
        for ahead in range(1, STACK):
            part_y_copy(plane, ahead).start()

        @pl.when(step + 1 < PLANES)
        def _():
            z_landed(step + 1).wait_recv()
            core_copy(around(-offset_of(step + 1)), core).start()

    def halfway(step):
        plane = around(-offset_of(step))
        part_x_copy(plane).wait_recv()
        mid_x[plane] = (
            part[plane, x_lo, :, :, left].astype(F32) + part_x[plane].astype(F32)
        ).astype(BF16)
        for ahead in range(1, STACK):
            mid_x_copy(plane, ahead).start()
        for ahead in range(1, STACK):
            part_y_copy(plane, ahead).wait_recv()

        def total(side):
            parts = [part_y[plane, slot, side].astype(F32) for slot in range(STACK - 1)]
            return part[plane, side, y, :, right].astype(F32) + parts[0] + parts[1] + parts[2]

        mid_y[plane] = total(1 - x_lo).astype(BF16)
        mid_y_copy(plane).start()
        keep_y[plane] = total(x_lo)

    def gelu(inner):
        return (0.5 * inner * (1.0 + lax.erf(inner * math.sqrt(0.5)))).astype(BF16)

    def collect(step):
        plane = around(-offset_of(step))
        for ahead in range(1, STACK):
            mid_x_copy(plane, ahead).wait_recv()
        total = mid_x[plane, y].astype(F32)
        for slot in range(STACK - 1):
            total += fin_x[plane, slot].astype(F32)
        strips[plane] = total[:, : 3 * HEAD].astype(BF16).astype(F32)
        cut = X_FIRST - 3 * HEAD
        acts[plane, x_lo, y, :, HEAD : HEAD + cut] = gelu(total[:, 3 * HEAD :] + bias[:, :cut])
        mid_y_copy(plane).wait_recv()
        total = keep_y[plane] + fin_y[plane].astype(F32)
        acts[plane, x_lo, y, :, HEAD + cut :] = gelu(total + bias[:, cut:])

    bias_copy = weights[6]
    bias_copy.wait()

    def first_half(step, carry):
        @pl.when(step < PLANES)
        def _():
            project(step)

        @pl.when((step >= LAG) & (step < PLANES + LAG))
        def _():
            halfway(step - LAG)

        @pl.when(step >= 2 * LAG)
        def _():
            collect(step - 2 * LAG)

        return carry

    lax.fori_loop(0, PLANES + 2 * LAG, first_half, 0)

    whole = strips[...].reshape(BLOCK, 3 * HEAD)
    query_norm = normalize(whole[:, :HEAD]).astype(BF16)
    key_norm = normalize(whole[:, HEAD : 2 * HEAD]).astype(BF16)
    scores = lax.dot_general(
        query_norm, key_norm, (((1,), (1,)), ((), ())), preferred_element_type=F32
    ) * (temper[...] / math.sqrt(HEAD))
    weight = jnp.exp(scores - jnp.max(scores, axis=-1, keepdims=True))
    probs = (weight / jnp.sum(weight, axis=-1, keepdims=True)).astype(BF16)
    mixed = jnp.dot(probs, whole[:, 2 * HEAD :].astype(BF16), preferred_element_type=F32)
    mixed = mixed.astype(BF16).reshape(PLANES, STRIP, HEAD)
    for plane in range(PLANES):
        acts[plane, x_lo, y, :, :HEAD] = mixed[plane]

    early, late = pl.ds(0, X_ACTS), pl.ds(X_ACTS, SECOND - X_ACTS)

    def acts_x_copy(plane, side):
        place = acts.at[plane, side, y, :, early]
        return send(place, place, acts_sem, (plane, 0), other_x_lo)

    def acts_y_copy(plane, step):
        place = acts.at[plane, x_lo, y]
        return send(place, place, acts_sem, (plane, step), y_device(y_at(step)))

    def acts_y_landed(plane, step):
        place = acts.at[plane, x_lo, y_before(step)]
        return send(place, place, acts_sem, (plane, step), y_device(y_before(step)))

    def pass_y_copy(plane, step):
        place = acts.at[plane, 1 - x_lo, y, :, early]
        return send(place, place, acts_sem, (plane, 3 + step), y_device(y_at(step)))

    def pass_y_landed(plane, step):
        place = acts.at[plane, 1 - x_lo, y_before(step), :, early]
        return send(place, place, acts_sem, (plane, 3 + step), y_device(y_before(step)))

    def pass_x_copy(plane, side):
        place = acts.at[plane, side, :, :, late]
        return send(place, place, acts_sem, (plane, 7), other_x_lo)

    def spread(step):
        plane = around(offset_of(PLANES - 1 - step))
        acts_x_copy(plane, x_lo).start()
        for ahead in range(1, STACK):
            acts_y_copy(plane, ahead).start()

    def pass_on(step):
        plane = around(offset_of(PLANES - 1 - step))
        acts_x_copy(plane, 1 - x_lo).wait_recv()
        for ahead in range(1, STACK):
            pass_y_copy(plane, ahead).start()
        for ahead in range(1, STACK):
            acts_y_landed(plane, ahead).wait_recv()
        pass_x_copy(plane, x_lo).start()

    def pair_copy(plane):
        return send(pair_out.at[plane], pair_in.at[plane], pair_sem, (plane,), other_core)

    def plane_copy(plane, slot):
        return send(plane_out.at[plane], plane_in.at[slot], plane_sem, (slot,), plane_device(plane))

    def plane_landed(slot):
        place = plane_in.at[slot]
        return send(place, place, plane_sem, (slot,), plane_device(around(-offset_of(slot + 1))))

    def output(step):
        plane = around(offset_of(PLANES - 1 - step))
        for ahead in range(1, STACK):
            pass_y_landed(plane, ahead).wait_recv()
        pass_x_copy(plane, 1 - x_lo).wait_recv()
        rows = jnp.dot(
            from_strips(), acts[plane].reshape(BLOCK, SECOND), preferred_element_type=F32
        ).astype(BF16)
        block = jnp.dot(rows, second[...], preferred_element_type=F32).reshape(2, 64, WIDTH)
        pair_out[plane] = jnp.where(core == 0, block[1], block[0]).astype(BF16)
        pair_copy(plane).start()
        pair_own[plane] = jnp.where(core == 0, block[0], block[1])

    def merge(step):
        slot = PLANES - 2 - step
        plane = around(offset_of(slot + 1))
        pair_copy(plane).wait_recv()
        total = pair_own[plane] + pair_in[plane].astype(F32)

        @pl.when(slot >= 0)
        def _():
            plane_out[plane] = total.astype(BF16)
            plane_copy(plane, slot).start()

        @pl.when(slot < 0)
        def _():
            pair_own[plane] = total

    for copy in weights[7:]:
        copy.wait()

    def second_half(step, carry):
        @pl.when(step < PLANES)
        def _():
            spread(step)

        @pl.when((step >= LAG) & (step < PLANES + LAG))
        def _():
            pass_on(step - LAG)

        @pl.when((step >= 2 * LAG) & (step < PLANES + 2 * LAG))
        def _():
            output(step - 2 * LAG)

        @pl.when(step >= 2 * LAG + 1)
        def _():
            merge(step - 2 * LAG - 1)

        return carry

    lax.fori_loop(0, PLANES + 2 * LAG + 1, second_half, 0)
    total = pair_own[z]
    for slot in reversed(range(PLANES - 1)):
        plane_landed(slot).wait_recv()
        total += plane_in[slot].astype(F32)
    lines[...] = total
    for side in range(2):
        for image in range(IMAGES):
            final_out[side, image] = lines[pl.ds(side * 32 + image * ROWS, ROWS), :].astype(BF16)

    def final_copy(step, flip):
        return send(
            final_out.at[half(flip), image_at(step)],
            final_in.at[dp, x_hi],
            final_sem,
            (step, flip),
            (image_at(step), half_mp(flip)),
        )

    def final_landed(step, flip):
        place = final_in.at[image_before(step), half(flip)]
        return send(place, place, final_sem, (step, flip), (image_before(step), half_mp(flip)))

    for piece in pieces:
        final_copy(*piece).start()
    final_in[dp, x_hi] = final_out[x_hi, dp]
    for piece in pieces:
        final_landed(*piece).wait_recv()
    for block in range(IMAGES):
        columns = pl.ds(block * WIDTH, WIDTH)
        total = final_in[block, 0].astype(F32) + final_in[block, 1].astype(F32)
        out[:, columns] = (tokens[:, columns].astype(F32) + total).astype(BF16)

    for piece in pieces:
        norm_copy(*piece).wait_send()
        final_copy(*piece).wait_send()
    for step in range(1, PLANES):
        z_copy(step).wait_send()
        plane_copy(around(offset_of(step)), step - 1).wait_send()

    def sent(plane, carry):
        core_copy(plane, core).wait_send()
        pair_copy(plane).wait_send()
        part_x_copy(plane).wait_send()
        mid_y_copy(plane).wait_send()
        acts_x_copy(plane, x_lo).wait_send()
        pass_x_copy(plane, x_lo).wait_send()
        for ahead in range(1, STACK):
            part_y_copy(plane, ahead).wait_send()
            mid_x_copy(plane, ahead).wait_send()
            acts_y_copy(plane, ahead).wait_send()
            pass_y_copy(plane, ahead).wait_send()
        return carry

    lax.fori_loop(0, PLANES, sent, 0)


def per_device(
    tokens, norm_gain, w_query, w_key, w_value, w_inner, bias_inner, w_attn_out, w_outer, temper
):
    vmem = pl.BlockSpec(memory_space=pltpu.VMEM)
    anywhere = pl.BlockSpec(memory_space=pl.ANY)
    dma = pltpu.SemaphoreType.DMA
    return pl.pallas_call(
        kernel,
        out_shape=jax.ShapeDtypeStruct(tokens.shape, BF16),
        in_specs=[anywhere] * 9 + [vmem],
        out_specs=vmem,
        scratch_shapes=[
            pltpu.VMEM((ROWS, IMAGES * WIDTH), BF16),
            pltpu.VMEM((1, IMAGES * WIDTH), F32),
            pltpu.VMEM((1, HIDDEN), F32),
            pltpu.VMEM((WIDTH, FIRST), BF16),
            pltpu.VMEM((SECOND, WIDTH), BF16),
            pltpu.VMEM((IMAGES, ROWS, WIDTH), BF16),
            pltpu.VMEM((IMAGES, 2, ROWS, WIDTH), BF16),
            pltpu.VMEM((64, WIDTH), F32),
            pltpu.VMEM((PLANES, 2, 64, WIDTH), BF16),
            pltpu.VMEM((PLANES, 2, STACK, STRIP, FIRST), BF16),
            pltpu.VMEM((PLANES, STACK, STRIP, X_FIRST), BF16),
            pltpu.VMEM((PLANES, STACK, STRIP, X_FIRST), BF16),
            pltpu.VMEM((PLANES, STACK - 1, STRIP, X_FIRST), BF16),
            pltpu.VMEM((PLANES, STACK - 1, 2, STRIP, Y_FIRST), BF16),
            pltpu.VMEM((PLANES, STRIP, Y_FIRST), BF16),
            pltpu.VMEM((PLANES, STRIP, Y_FIRST), F32),
            pltpu.VMEM((PLANES, STRIP, Y_FIRST), BF16),
            pltpu.VMEM((PLANES, STRIP, 3 * HEAD), F32),
            pltpu.VMEM((PLANES, 2, STACK, STRIP, SECOND), BF16),
            pltpu.VMEM((PLANES, 64, WIDTH), F32),
            pltpu.VMEM((PLANES, 64, WIDTH), BF16),
            pltpu.VMEM((PLANES, 64, WIDTH), BF16),
            pltpu.VMEM((PLANES, 64, WIDTH), BF16),
            pltpu.VMEM((PLANES - 1, 64, WIDTH), BF16),
            pltpu.VMEM((2, IMAGES, ROWS, WIDTH), BF16),
            pltpu.VMEM((IMAGES, 2, ROWS, WIDTH), BF16),
            dma((9,)),
            dma((2, IMAGES, 2)),
            dma((2, PLANES)),
            dma((2, PLANES)),
            dma((2, PLANES, 8)),
            dma((2, PLANES, 8)),
            dma((2, PLANES)),
            dma((2, PLANES - 1)),
            dma((2, IMAGES, 2)),
        ],
        compiler_params=pltpu.CompilerParams(
            collective_id=0, has_side_effects=True, vmem_limit_bytes=67043328
        ),
    )(
        tokens,
        norm_gain.reshape(1, -1),
        w_query,
        w_key,
        w_value,
        w_inner,
        bias_inner.reshape(1, -1),
        w_attn_out,
        w_outer,
        temper.reshape(1, 1),
    )


def solution(mesh):
    return jax.shard_map(
        per_device,
        mesh=mesh,
        in_specs=(
            P(("dp", "mp"), None),
            P(),
            P("dp", "mp"),
            P("dp", "mp"),
            P("dp", "mp"),
            P("dp", "mp"),
            P("mp"),
            P("mp", "dp"),
            P("mp", "dp"),
            P("mp"),
        ),
        out_specs=P(("dp", "mp"), None),
        check_vma=False,
    )
```

time: 104 us -> 87.2 us (0.84)
  Pallas kernels: 93.5 us -> 82.5 us
  local copies, waits for them, and re-layouts: 9.09 us -> 2.7 us
    pallas_call x1, Pallas kernels: 93.5 us -> 82.5 us  [per_device(): pl.pallas_call(kernel, out_shape=jax.ShapeDtypeStruct(tokens.shape, BF16)...]
    unnamed x17 -> x1, local copies, waits for them, and re-layouts: 8.4 us -> 1.44 us
where the time goes in v2:
time: 87.2 us; the launch traced here: 85.8 us
  Pallas kernels  82.5 us (95%)
  local copies, waits for them, and re-layouts  2.7 us (3%)
    pallas_call x1, Pallas kernels, per_device(): pl.pallas_call(kernel, out_shape=jax.ShapeDtypeStruct(tokens.shape, BF16)...  82.5 us

profile of v2, /device:TPU:8, one launch (start us, length us, event | category | flops | bytes accessed | tf_op | source)
XLA Modules:
  0.0 85.8 jit_solution(11485369768245077406)
XLA Ops:
  0.7 1.3 %reshape.10.bias_hbm = f32[1,768]{1,0:T(1,128)} reshape(f32[768]{0:T(1024)} %param.16) | data formatting | bytes 6144 | tf_op jit(solution)/shard_map/reshape | solution.py:553
  1.9 82.5 %shard_map.100 = bf16[4,6144]{1,0:T(4,128)(2,1)} custom-call(bf16[4,6144]{1,0:T(4,128)(2,1)} %tokens_hbm.1, f32[1,6144]{1,0:T(1,128)} %bitcast.3, bf16[768,128]{1,0:T(8,128)(2,1)} %w_query.1, bf16[768,128]{1,0:T(8,128)(2,1)} %w_key.1, bf16[768,128]{1,0:T(8,128)(2,1)} %w_value.1, bf16[768,768]{1,0:T(8,128)(2,1)} %w_inner.1, f32[1,768]{1,0:T(1,128)} %reshape.10.bias_hbm, ...), custom_call_target="tpu_custom_call" | custom-call | tf_op jit(solution)/shard_map/pallas_call | solution.py:501
  84.4 1.4 %copy.13 = bf16[4,6144]{1,0:T(4,128)(2,1)} copy(bf16[4,6144]{1,0:T(4,128)(2,1)} %shard_map.100) | data formatting | bytes 98304

commit v3 on v2

--- a/solution.py
+++ b/solution.py
@@ -64,11 +64,12 @@
     bias_hbm,
     w_attn_out,
     w_outer,
-    temper,
+    temper_hbm,
     out,
     tokens,
     gain,
     bias,
+    temper,
     first,
     second,
     norm_out,
@@ -88,8 +89,8 @@
     pair_own,
     pair_out,
     pair_in,
-    plane_out,
-    plane_in,
+    ring_out,
+    ring_in,
     final_out,
     final_in,
     w_sem,
@@ -99,7 +100,7 @@
     part_sem,
     acts_sem,
     pair_sem,
-    plane_sem,
+    ring_sem,
     final_sem,
 ):
     dp = lax.axis_index("dp")
@@ -149,6 +150,7 @@
         pltpu.make_async_copy(w_value, first.at[:, pl.ds(2 * HEAD, HEAD)], w_sem.at[2]),
         pltpu.make_async_copy(w_inner, first.at[:, pl.ds(3 * HEAD, HIDDEN)], w_sem.at[3]),
         pltpu.make_async_copy(bias_hbm, bias, w_sem.at[8]),
+        pltpu.make_async_copy(temper_hbm, temper, w_sem.at[9]),
         pltpu.make_async_copy(w_attn_out, second.at[pl.ds(0, HEAD), :], w_sem.at[4]),
         pltpu.make_async_copy(w_outer, second.at[pl.ds(HEAD, HIDDEN), :], w_sem.at[5]),
     ]
@@ -163,8 +165,8 @@
         return z * 4 + half(flip) * 2 + core
 
     barrier = pltpu.get_barrier_semaphore()
-    peers = [plane_device(around(offset_of(step))) for step in reversed(range(1, PLANES))]
-    peers += [(image_at(step), half_mp(flip)) for step, flip in pieces] + [other_core]
+    peers = [(image_at(step), half_mp(flip)) for step, flip in pieces]
+    peers += [plane_device(around(1)), plane_device(around(-1)), other_core]
     for peer in peers:
         pl.semaphore_signal(barrier, inc=1, device_id=peer, device_id_type=MESH)
     for copy in weights[2:]:
@@ -200,21 +202,31 @@
             lines[pl.ds(side * 32 + image * ROWS, ROWS), :] = norm_in[image, side].astype(F32)
     planes[z, core] = lines[...].astype(BF16)
 
+    def z_way(step):
+        return 2 * (step % 2) - 1
+
     def z_copy(step):
-        place = planes.at[z, core]
-        return send(place, place, z_sem, (step,), plane_device(around(offset_of(step))))
+        place = planes.at[around(z_way(step) - offset_of(step)), core]
+        return send(place, place, z_sem, (step,), plane_device(around(z_way(step))))
+
+    def z_half_copy(side):
+        place = planes.at[around(-3 + 6 * side), core, pl.ds(32 * side, 32)]
+        return send(place, place, z_sem, (7 + side,), plane_device(around(1 - 2 * side)))
 
     def z_landed(step):
-        plane = around(-offset_of(step))
-        place = planes.at[plane, core]
-        return send(place, place, z_sem, (step,), plane_device(plane))
+        place = planes.at[around(-offset_of(step)), core]
+        return send(place, place, z_sem, (step,), plane_device(around(-z_way(step))))
+
+    def z_half_landed(side):
+        place = planes.at[around(4), core, pl.ds(32 * side, 32)]
+        return send(place, place, z_sem, (7 + side,), plane_device(around(2 * side - 1)))
 
     def core_copy(plane, side):
         place = planes.at[plane, side]
         return send(place, place, core_sem, (plane,), other_core)
 
     core_copy(z, core).start()
-    for step in range(1, PLANES):
+    for step in (1, 2):
         z_copy(step).start()
     for copy in weights[2:6]:
         copy.wait()
@@ -262,8 +274,28 @@
 
         @pl.when(step + 1 < PLANES)
         def _():
-            z_landed(step + 1).wait_recv()
-            core_copy(around(-offset_of(step + 1)), core).start()
+            arrival = step + 1
+
+            @pl.when(arrival < 7)
+            def _():
+                z_landed(arrival).wait_recv()
+
+            @pl.when(arrival == 7)
+            def _():
+                for side in range(2):
+                    z_half_landed(side).wait_recv()
+
+            @pl.when(arrival < 5)
+            def _():
+                z_copy(arrival + 2).start()
+
+            for side in range(2):
+
+                @pl.when(arrival == 5 + side)
+                def _():
+                    z_half_copy(side).start()
+
+            core_copy(around(-offset_of(arrival)), core).start()
 
     def halfway(step):
         plane = around(-offset_of(step))
@@ -296,13 +328,13 @@
             total += fin_x[plane, slot].astype(F32)
         strips[plane] = total[:, : 3 * HEAD].astype(BF16).astype(F32)
         cut = X_FIRST - 3 * HEAD
-        acts[plane, x_lo, y, :, HEAD : HEAD + cut] = gelu(total[:, 3 * HEAD :] + bias[:, :cut])
+        acts[plane, x_lo, y, :, HEAD : HEAD + cut] = gelu(total[:, 3 * HEAD :] + bias[:cut])
         mid_y_copy(plane).wait_recv()
         total = keep_y[plane] + fin_y[plane].astype(F32)
-        acts[plane, x_lo, y, :, HEAD + cut :] = gelu(total + bias[:, cut:])
-
-    bias_copy = weights[6]
-    bias_copy.wait()
+        acts[plane, x_lo, y, :, HEAD + cut :] = gelu(total + bias[cut:])
+
+    for copy in weights[6:8]:
+        copy.wait()
 
     def first_half(step, carry):
         @pl.when(step < PLANES)
@@ -326,7 +358,7 @@
     key_norm = normalize(whole[:, HEAD : 2 * HEAD]).astype(BF16)
     scores = lax.dot_general(
         query_norm, key_norm, (((1,), (1,)), ((), ())), preferred_element_type=F32
-    ) * (temper[...] / math.sqrt(HEAD))
+    ) * (temper[...].reshape(1, 1) / math.sqrt(HEAD))
     weight = jnp.exp(scores - jnp.max(scores, axis=-1, keepdims=True))
     probs = (weight / jnp.sum(weight, axis=-1, keepdims=True)).astype(BF16)
     mixed = jnp.dot(probs, whole[:, 2 * HEAD :].astype(BF16), preferred_element_type=F32)
@@ -378,12 +410,21 @@
     def pair_copy(plane):
         return send(pair_out.at[plane], pair_in.at[plane], pair_sem, (plane,), other_core)
 
-    def plane_copy(plane, slot):
-        return send(plane_out.at[plane], plane_in.at[slot], plane_sem, (slot,), plane_device(plane))
-
-    def plane_landed(slot):
-        place = plane_in.at[slot]
-        return send(place, place, plane_sem, (slot,), plane_device(around(-offset_of(slot + 1))))
+    def ring_copy(step):
+        return send(ring_out.at[step], ring_in.at[step], ring_sem, (step,), plane_device(around(-z_way(step))))
+
+    def ring_landed(step):
+        return send(ring_in.at[step], ring_in.at[step], ring_sem, (step,), plane_device(around(z_way(step))))
+
+    def ring_half_copy(side):
+        rows = pl.ds(32 * side, 32)
+        return send(
+            ring_out.at[0, rows], ring_in.at[0, rows], ring_sem, (7 * side,), plane_device(around(1 - 2 * side))
+        )
+
+    def ring_half_landed(side):
+        place = ring_in.at[0, pl.ds(32 * side, 32)]
+        return send(place, place, ring_sem, (7 * side,), plane_device(around(2 * side - 1)))
 
     def output(step):
         plane = around(offset_of(PLANES - 1 - step))
@@ -399,21 +440,36 @@
         pair_own[plane] = jnp.where(core == 0, block[0], block[1])
 
     def merge(step):
-        slot = PLANES - 2 - step
-        plane = around(offset_of(slot + 1))
+        plane = around(offset_of(PLANES - 1 - step))
         pair_copy(plane).wait_recv()
-        total = pair_own[plane] + pair_in[plane].astype(F32)
-
-        @pl.when(slot >= 0)
-        def _():
-            plane_out[plane] = total.astype(BF16)
-            plane_copy(plane, slot).start()
-
-        @pl.when(slot < 0)
-        def _():
-            pair_own[plane] = total
-
-    for copy in weights[7:]:
+        pair_own[plane] = pair_own[plane] + pair_in[plane].astype(F32)
+        for side in range(2):
+
+            @pl.when(step == 2 - side)
+            def _():
+                rows = pl.ds(32 * side, 32)
+                ring_half_landed(side).wait_recv()
+                pair_own[plane, rows] = pair_own[plane, rows] + ring_in[0, rows].astype(F32)
+
+        @pl.when(step >= 3)
+        def _():
+            ring_landed(step - 2).wait_recv()
+            pair_own[plane] = pair_own[plane] + ring_in[step - 2].astype(F32)
+
+        @pl.when(step < PLANES - 1)
+        def _():
+            ring_out[step] = pair_own[plane].astype(BF16)
+
+        @pl.when(step == 0)
+        def _():
+            for side in range(2):
+                ring_half_copy(side).start()
+
+        @pl.when((step > 0) & (step < PLANES - 1))
+        def _():
+            ring_copy(step).start()
+
+    for copy in weights[8:]:
         copy.wait()
 
     def second_half(step, carry):
@@ -436,11 +492,8 @@
         return carry
 
     lax.fori_loop(0, PLANES + 2 * LAG + 1, second_half, 0)
-    total = pair_own[z]
-    for slot in reversed(range(PLANES - 1)):
-        plane_landed(slot).wait_recv()
-        total += plane_in[slot].astype(F32)
-    lines[...] = total
+    ring_landed(6).wait_recv()
+    lines[...] = pair_own[z] + ring_in[6].astype(F32)
     for side in range(2):
         for image in range(IMAGES):
             final_out[side, image] = lines[pl.ds(side * 32 + image * ROWS, ROWS), :].astype(BF16)
@@ -471,9 +524,12 @@
     for piece in pieces:
         norm_copy(*piece).wait_send()
         final_copy(*piece).wait_send()
-    for step in range(1, PLANES):
+    for step in range(1, 7):
         z_copy(step).wait_send()
-        plane_copy(around(offset_of(step)), step - 1).wait_send()
+        ring_copy(step).wait_send()
+    for side in range(2):
+        z_half_copy(side).wait_send()
+        ring_half_copy(side).wait_send()
 
     def sent(plane, carry):
         core_copy(plane, core).wait_send()
@@ -496,17 +552,18 @@
     tokens, norm_gain, w_query, w_key, w_value, w_inner, bias_inner, w_attn_out, w_outer, temper
 ):
     vmem = pl.BlockSpec(memory_space=pltpu.VMEM)
-    anywhere = pl.BlockSpec(memory_space=pl.ANY)
+    hbm = pl.BlockSpec(memory_space=pltpu.HBM)
     dma = pltpu.SemaphoreType.DMA
     return pl.pallas_call(
         kernel,
         out_shape=jax.ShapeDtypeStruct(tokens.shape, BF16),
-        in_specs=[anywhere] * 9 + [vmem],
+        in_specs=[hbm] * 10,
         out_specs=vmem,
         scratch_shapes=[
             pltpu.VMEM((ROWS, IMAGES * WIDTH), BF16),
             pltpu.VMEM((1, IMAGES * WIDTH), F32),
-            pltpu.VMEM((1, HIDDEN), F32),
+            pltpu.VMEM((HIDDEN,), F32),
+            pltpu.VMEM((1,), F32),
             pltpu.VMEM((WIDTH, FIRST), BF16),
             pltpu.VMEM((SECOND, WIDTH), BF16),
             pltpu.VMEM((IMAGES, ROWS, WIDTH), BF16),
@@ -526,18 +583,18 @@
             pltpu.VMEM((PLANES, 64, WIDTH), F32),
             pltpu.VMEM((PLANES, 64, WIDTH), BF16),
             pltpu.VMEM((PLANES, 64, WIDTH), BF16),
-            pltpu.VMEM((PLANES, 64, WIDTH), BF16),
+            pltpu.VMEM((PLANES - 1, 64, WIDTH), BF16),
             pltpu.VMEM((PLANES - 1, 64, WIDTH), BF16),
             pltpu.VMEM((2, IMAGES, ROWS, WIDTH), BF16),
             pltpu.VMEM((IMAGES, 2, ROWS, WIDTH), BF16),
-            dma((9,)),
+            dma((10,)),
             dma((2, IMAGES, 2)),
-            dma((2, PLANES)),
+            dma((2, 9)),
             dma((2, PLANES)),
             dma((2, PLANES, 8)),
             dma((2, PLANES, 8)),
             dma((2, PLANES)),
-            dma((2, PLANES - 1)),
+            dma((2, PLANES)),
             dma((2, IMAGES, 2)),
         ],
         compiler_params=pltpu.CompilerParams(
@@ -550,10 +607,10 @@
         w_key,
         w_value,
         w_inner,
-        bias_inner.reshape(1, -1),
+        bias_inner,
         w_attn_out,
         w_outer,
-        temper.reshape(1, 1),
+        temper,
     )
 
 

time: 87.2 us -> 79 us (0.906); the launches traced: 85.8 us -> 78.8 us
  Pallas kernels: 82.5 us -> 76.7 us
  local copies, waits for them, and re-layouts: 2.7 us -> 1.44 us
    pallas_call x1, Pallas kernels: 82.5 us -> 76.7 us  [per_device(): pl.pallas_call(kernel, out_shape=jax.ShapeDtypeStruct(tokens.shape, BF16)...]
    reshape x1 -> x0, local copies, waits for them, and re-layouts: 1.27 us -> none  [per_device(): bias_inner.reshape(1, -1)]
where the time goes in v3:
time: 79 us; the launch traced here: 78.8 us
  Pallas kernels  76.7 us (97%)
  local copies, waits for them, and re-layouts  1.44 us (2%)
    pallas_call x1, Pallas kernels, per_device(): pl.pallas_call(kernel, out_shape=jax.ShapeDtypeStruct(tokens.shape, BF16)...  76.7 us

profile of v3, /device:TPU:8, one launch (start us, length us, event | category | flops | bytes accessed | tf_op | source)
XLA Modules:
  0.0 78.8 jit_solution(950847493652806639)
XLA Ops:
  0.7 76.7 %shard_map.100 = bf16[4,6144]{1,0:T(4,128)(2,1)} custom-call(bf16[4,6144]{1,0:T(4,128)(2,1)} %tokens_hbm.1, f32[1,6144]{1,0:T(1,128)} %bitcast.1, bf16[768,128]{1,0:T(8,128)(2,1)} %w_query.1, bf16[768,128]{1,0:T(8,128)(2,1)} %w_key.1, bf16[768,128]{1,0:T(8,128)(2,1)} %w_value.1, bf16[768,768]{1,0:T(8,128)(2,1)} %w_inner.1, f32[768]{0:T(1024)} %bias_hbm.1, ...), custom_call_target="tpu_custom_call" | custom-call | tf_op jit(solution)/shard_map/pallas_call | solution.py:557
  77.4 1.4 %copy.13 = bf16[4,6144]{1,0:T(4,128)(2,1)} copy(bf16[4,6144]{1,0:T(4,128)(2,1)} %shard_map.100) | data formatting | bytes 98304

commit v4 on v3

--- a/solution.py
+++ b/solution.py
@@ -21,7 +21,8 @@
 Y_FIRST = FIRST - X_FIRST
 SECOND = HEAD + HIDDEN
 LAG = 2
-X_ACTS = 512
+X_ACTS = 384
+AHEAD = 3
 MESH = pl.DeviceIdType.MESH
 F32 = jnp.float32
 BF16 = jnp.bfloat16
@@ -99,6 +100,7 @@
     core_sem,
     part_sem,
     acts_sem,
+    mixed_sem,
     pair_sem,
     ring_sem,
     final_sem,
@@ -336,14 +338,70 @@
     for copy in weights[6:8]:
         copy.wait()
 
+    hidden = pl.ds(HEAD, HIDDEN)
+    early, late = pl.ds(HEAD, X_ACTS), pl.ds(HEAD + X_ACTS, HIDDEN - X_ACTS)
+
+    def mixed_copy(step):
+        place = acts.at[:, x_lo, y, :, pl.ds(0, HEAD)]
+        return send(place, place, mixed_sem, (step,), (image_at(step), mp))
+
+    def mixed_landed(step):
+        image = image_before(step)
+        place = acts.at[:, image // STACK, image % STACK, :, pl.ds(0, HEAD)]
+        return send(place, place, mixed_sem, (step,), (image, mp))
+
+    def acts_x_copy(plane, side):
+        place = acts.at[plane, side, y, :, early]
+        return send(place, place, acts_sem, (plane, 0), other_x_lo)
+
+    def acts_y_copy(plane, step):
+        place = acts.at[plane, x_lo, y, :, hidden]
+        return send(place, place, acts_sem, (plane, step), y_device(y_at(step)))
+
+    def acts_y_landed(plane, step):
+        place = acts.at[plane, x_lo, y_before(step), :, hidden]
+        return send(place, place, acts_sem, (plane, step), y_device(y_before(step)))
+
+    def pass_y_copy(plane, step):
+        place = acts.at[plane, 1 - x_lo, y, :, early]
+        return send(place, place, acts_sem, (plane, 3 + step), y_device(y_at(step)))
+
+    def pass_y_landed(plane, step):
+        place = acts.at[plane, 1 - x_lo, y_before(step), :, early]
+        return send(place, place, acts_sem, (plane, 3 + step), y_device(y_before(step)))
+
+    def pass_x_copy(plane, side):
+        place = acts.at[plane, side, :, :, late]
+        return send(place, place, acts_sem, (plane, 7), other_x_lo)
+
+    def spread(step):
+        plane = around(offset_of(PLANES - 1 - step))
+        acts_x_copy(plane, x_lo).start()
+        for ahead in range(1, STACK):
+            acts_y_copy(plane, ahead).start()
+
+    def pass_on(step):
+        plane = around(offset_of(PLANES - 1 - step))
+        acts_x_copy(plane, 1 - x_lo).wait_recv()
+        for ahead in range(1, STACK):
+            pass_y_copy(plane, ahead).start()
+        for ahead in range(1, STACK):
+            acts_y_landed(plane, ahead).wait_recv()
+        pass_x_copy(plane, x_lo).start()
+
     def first_half(step, carry):
+        @pl.when((step >= LAG) & (step < PLANES + LAG))
+        def _():
+            halfway(step - LAG)
+
+        @pl.when(step == PLANES + LAG - 1)
+        def _():
+            for behind in range(AHEAD):
+                spread(PLANES - 1 - behind)
+
         @pl.when(step < PLANES)
         def _():
             project(step)
-
-        @pl.when((step >= LAG) & (step < PLANES + LAG))
-        def _():
-            halfway(step - LAG)
 
         @pl.when(step >= 2 * LAG)
         def _():
@@ -365,47 +423,8 @@
     mixed = mixed.astype(BF16).reshape(PLANES, STRIP, HEAD)
     for plane in range(PLANES):
         acts[plane, x_lo, y, :, :HEAD] = mixed[plane]
-
-    early, late = pl.ds(0, X_ACTS), pl.ds(X_ACTS, SECOND - X_ACTS)
-
-    def acts_x_copy(plane, side):
-        place = acts.at[plane, side, y, :, early]
-        return send(place, place, acts_sem, (plane, 0), other_x_lo)
-
-    def acts_y_copy(plane, step):
-        place = acts.at[plane, x_lo, y]
-        return send(place, place, acts_sem, (plane, step), y_device(y_at(step)))
-
-    def acts_y_landed(plane, step):
-        place = acts.at[plane, x_lo, y_before(step)]
-        return send(place, place, acts_sem, (plane, step), y_device(y_before(step)))
-
-    def pass_y_copy(plane, step):
-        place = acts.at[plane, 1 - x_lo, y, :, early]
-        return send(place, place, acts_sem, (plane, 3 + step), y_device(y_at(step)))
-
-    def pass_y_landed(plane, step):
-        place = acts.at[plane, 1 - x_lo, y_before(step), :, early]
-        return send(place, place, acts_sem, (plane, 3 + step), y_device(y_before(step)))
-
-    def pass_x_copy(plane, side):
-        place = acts.at[plane, side, :, :, late]
-        return send(place, place, acts_sem, (plane, 7), other_x_lo)
-
-    def spread(step):
-        plane = around(offset_of(PLANES - 1 - step))
-        acts_x_copy(plane, x_lo).start()
-        for ahead in range(1, STACK):
-            acts_y_copy(plane, ahead).start()
-
-    def pass_on(step):
-        plane = around(offset_of(PLANES - 1 - step))
-        acts_x_copy(plane, 1 - x_lo).wait_recv()
-        for ahead in range(1, STACK):
-            pass_y_copy(plane, ahead).start()
-        for ahead in range(1, STACK):
-            acts_y_landed(plane, ahead).wait_recv()
-        pass_x_copy(plane, x_lo).start()
+    for step in range(1, IMAGES):
+        mixed_copy(step).start()
 
     def pair_copy(plane):
         return send(pair_out.at[plane], pair_in.at[plane], pair_sem, (plane,), other_core)
@@ -473,21 +492,30 @@
         copy.wait()
 
     def second_half(step, carry):
-        @pl.when(step < PLANES)
+        @pl.when(step < PLANES - AHEAD)
         def _():
             spread(step)
 
-        @pl.when((step >= LAG) & (step < PLANES + LAG))
+        @pl.when(step < AHEAD)
+        def _():
+            pass_on(PLANES - AHEAD + step)
+
+        @pl.when((step >= LAG) & (step < PLANES - AHEAD + LAG))
         def _():
             pass_on(step - LAG)
 
+        @pl.when(step == 2 * LAG)
+        def _():
+            for ahead in range(1, IMAGES):
+                mixed_landed(ahead).wait_recv()
+
+        @pl.when(step >= 2 * LAG + 1)
+        def _():
+            merge(step - 2 * LAG - 1)
+
         @pl.when((step >= 2 * LAG) & (step < PLANES + 2 * LAG))
         def _():
             output(step - 2 * LAG)
-
-        @pl.when(step >= 2 * LAG + 1)
-        def _():
-            merge(step - 2 * LAG - 1)
 
         return carry
 
@@ -521,6 +549,8 @@
         total = final_in[block, 0].astype(F32) + final_in[block, 1].astype(F32)
         out[:, columns] = (tokens[:, columns].astype(F32) + total).astype(BF16)
 
+    for step in range(1, IMAGES):
+        mixed_copy(step).wait_send()
     for piece in pieces:
         norm_copy(*piece).wait_send()
         final_copy(*piece).wait_send()
@@ -593,6 +623,7 @@
             dma((2, PLANES)),
             dma((2, PLANES, 8)),
             dma((2, PLANES, 8)),
+            dma((2, IMAGES)),
             dma((2, PLANES)),
             dma((2, PLANES)),
             dma((2, IMAGES, 2)),

time: 79 us -> 85.6 us (1.084)
  Pallas kernels: 76.7 us -> 83.2 us
    pallas_call x1, Pallas kernels: 76.7 us -> 83.2 us  [per_device(): pl.pallas_call(kernel, out_shape=jax.ShapeDtypeStruct(tokens.shape, BF16)...]
where the time goes in v4:
time: 85.6 us; the launch traced here: 85.3 us
  Pallas kernels  83.2 us (97%)
  local copies, waits for them, and re-layouts  1.44 us (2%)
    pallas_call x1, Pallas kernels, per_device(): pl.pallas_call(kernel, out_shape=jax.ShapeDtypeStruct(tokens.shape, BF16)...  83.2 us

profile of v4, /device:TPU:8, one launch (start us, length us, event | category | flops | bytes accessed | tf_op | source)
XLA Modules:
  0.0 85.3 jit_solution(3286376585683951184)
XLA Ops:
  0.7 83.2 %shard_map.100 = bf16[4,6144]{1,0:T(4,128)(2,1)} custom-call(bf16[4,6144]{1,0:T(4,128)(2,1)} %tokens_hbm.1, f32[1,6144]{1,0:T(1,128)} %bitcast.1, bf16[768,128]{1,0:T(8,128)(2,1)} %w_query.1, bf16[768,128]{1,0:T(8,128)(2,1)} %w_key.1, bf16[768,128]{1,0:T(8,128)(2,1)} %w_value.1, bf16[768,768]{1,0:T(8,128)(2,1)} %w_inner.1, f32[768]{0:T(1024)} %bias_hbm.1, ...), custom_call_target="tpu_custom_call" | custom-call | tf_op jit(solution)/shard_map/pallas_call | solution.py:587
  83.8 1.4 %copy.13 = bf16[4,6144]{1,0:T(4,128)(2,1)} copy(bf16[4,6144]{1,0:T(4,128)(2,1)} %shard_map.100) | data formatting | bytes 98304

commit v5 on v4

--- a/solution.py
+++ b/solution.py
@@ -22,7 +22,11 @@
 SECOND = HEAD + HIDDEN
 LAG = 2
 X_ACTS = 384
-AHEAD = 3
+STRAIGHT = 2
+STAGED = PLANES - STRAIGHT
+AHEAD = 0
+SOON = 2
+FAR_FIRST = (2, 1, 3)
 MESH = pl.DeviceIdType.MESH
 F32 = jnp.float32
 BF16 = jnp.bfloat16
@@ -85,6 +89,7 @@
     mid_y,
     keep_y,
     fin_y,
+    straight_in,
     strips,
     acts,
     pair_own,
@@ -99,6 +104,7 @@
     z_sem,
     core_sem,
     part_sem,
+    straight_sem,
     acts_sem,
     mixed_sem,
     pair_sem,
@@ -168,7 +174,7 @@
 
     barrier = pltpu.get_barrier_semaphore()
     peers = [(image_at(step), half_mp(flip)) for step, flip in pieces]
-    peers += [plane_device(around(1)), plane_device(around(-1)), other_core]
+    peers += [plane_device(around(offset)) for offset in (1, -1)] + [other_core]
     for peer in peers:
         pl.semaphore_signal(barrier, inc=1, device_id=peer, device_id_type=MESH)
     for copy in weights[2:]:
@@ -261,18 +267,49 @@
     def mid_y_copy(plane):
         return send(mid_y.at[plane], fin_y.at[plane], part_sem, (plane, 7), other_x_lo)
 
+    def straight_copy(step, ahead):
+        image = image_at(ahead)
+        return send(
+            part.at[around(-offset_of(step)), image // STACK, image % STACK],
+            straight_in.at[step - STAGED, dp],
+            straight_sem,
+            (step - STAGED, ahead),
+            (image, mp),
+        )
+
+    def straight_landed(step, ahead):
+        image = image_before(ahead)
+        place = straight_in.at[step - STAGED, image]
+        return send(place, place, straight_sem, (step - STAGED, ahead), (image, mp))
+
     def project(step):
         plane = around(-offset_of(step))
         core_copy(plane, 1 - core).wait_recv()
         rows = jnp.dot(
             to_strips(), planes[plane].reshape(BLOCK, WIDTH), preferred_element_type=F32
         ).astype(BF16)
-        for columns, width in ((left, X_FIRST), (right, Y_FIRST)):
-            block = jnp.dot(rows, first[:, columns], preferred_element_type=F32)
-            part[plane, :, :, :, columns] = block.astype(BF16).reshape(2, STACK, STRIP, width)
-        part_x_copy(plane).start()
-        for ahead in range(1, STACK):
-            part_y_copy(plane, ahead).start()
+
+        def block(columns, width):
+            total = jnp.dot(rows, first[:, columns], preferred_element_type=F32)
+            part[plane, :, :, :, columns] = total.astype(BF16).reshape(2, STACK, STRIP, width)
+
+        block(left, X_FIRST)
+
+        @pl.when(step < STAGED)
+        def _():
+            part_x_copy(plane).start()
+
+        block(right, Y_FIRST)
+
+        @pl.when(step < STAGED)
+        def _():
+            for ahead in FAR_FIRST:
+                part_y_copy(plane, ahead).start()
+
+        @pl.when(step >= STAGED)
+        def _():
+            for ahead in range(1, IMAGES):
+                straight_copy(step, ahead).start()
 
         @pl.when(step + 1 < PLANES)
         def _():
@@ -305,7 +342,7 @@
         mid_x[plane] = (
             part[plane, x_lo, :, :, left].astype(F32) + part_x[plane].astype(F32)
         ).astype(BF16)
-        for ahead in range(1, STACK):
+        for ahead in FAR_FIRST:
             mid_x_copy(plane, ahead).start()
         for ahead in range(1, STACK):
             part_y_copy(plane, ahead).wait_recv()
@@ -335,73 +372,94 @@
         total = keep_y[plane] + fin_y[plane].astype(F32)
         acts[plane, x_lo, y, :, HEAD + cut :] = gelu(total + bias[cut:])
 
+    def collect_straight(step):
+        plane = around(-offset_of(step))
+        total = part[plane, x_lo, y].astype(F32)
+        for ahead in range(1, IMAGES):
+            straight_landed(step, ahead).wait_recv()
+            total += straight_in[step - STAGED, image_before(ahead)].astype(F32)
+        strips[plane] = total[:, : 3 * HEAD].astype(BF16).astype(F32)
+        acts[plane, x_lo, y, :, HEAD:] = gelu(total[:, 3 * HEAD :] + bias[...])
+
     for copy in weights[6:8]:
         copy.wait()
 
-    hidden = pl.ds(HEAD, HIDDEN)
-    early, late = pl.ds(HEAD, X_ACTS), pl.ds(HEAD + X_ACTS, HIDDEN - X_ACTS)
-
-    def mixed_copy(step):
-        place = acts.at[:, x_lo, y, :, pl.ds(0, HEAD)]
-        return send(place, place, mixed_sem, (step,), (image_at(step), mp))
-
-    def mixed_landed(step):
+    late = pl.ds(HEAD + X_ACTS, HIDDEN - X_ACTS)
+
+    def mixed_copy(plane, step):
+        place = acts.at[plane, x_lo, y, :, pl.ds(0, HEAD)]
+        return send(place, place, mixed_sem, (plane, step), (image_at(step), mp))
+
+    def mixed_landed(plane, step):
         image = image_before(step)
-        place = acts.at[:, image // STACK, image % STACK, :, pl.ds(0, HEAD)]
-        return send(place, place, mixed_sem, (step,), (image, mp))
-
-    def acts_x_copy(plane, side):
-        place = acts.at[plane, side, y, :, early]
+        place = acts.at[plane, image // STACK, image % STACK, :, pl.ds(0, HEAD)]
+        return send(place, place, mixed_sem, (plane, step), (image, mp))
+
+    def acts_x_copy(plane, side, low):
+        place = acts.at[plane, side, y, :, pl.ds(low, HEAD + X_ACTS - low)]
         return send(place, place, acts_sem, (plane, 0), other_x_lo)
 
-    def acts_y_copy(plane, step):
-        place = acts.at[plane, x_lo, y, :, hidden]
+    def acts_y_copy(plane, step, low):
+        place = acts.at[plane, x_lo, y, :, pl.ds(low, SECOND - low)]
         return send(place, place, acts_sem, (plane, step), y_device(y_at(step)))
 
-    def acts_y_landed(plane, step):
-        place = acts.at[plane, x_lo, y_before(step), :, hidden]
+    def acts_y_landed(plane, step, low):
+        place = acts.at[plane, x_lo, y_before(step), :, pl.ds(low, SECOND - low)]
         return send(place, place, acts_sem, (plane, step), y_device(y_before(step)))
 
-    def pass_y_copy(plane, step):
-        place = acts.at[plane, 1 - x_lo, y, :, early]
+    def pass_y_copy(plane, step, low):
+        place = acts.at[plane, 1 - x_lo, y, :, pl.ds(low, HEAD + X_ACTS - low)]
         return send(place, place, acts_sem, (plane, 3 + step), y_device(y_at(step)))
 
-    def pass_y_landed(plane, step):
-        place = acts.at[plane, 1 - x_lo, y_before(step), :, early]
+    def pass_y_landed(plane, step, low):
+        place = acts.at[plane, 1 - x_lo, y_before(step), :, pl.ds(low, HEAD + X_ACTS - low)]
         return send(place, place, acts_sem, (plane, 3 + step), y_device(y_before(step)))
 
     def pass_x_copy(plane, side):
         place = acts.at[plane, side, :, :, late]
         return send(place, place, acts_sem, (plane, 7), other_x_lo)
 
-    def spread(step):
-        plane = around(offset_of(PLANES - 1 - step))
-        acts_x_copy(plane, x_lo).start()
+    def far_first(step):
+        return around(offset_of(PLANES - 1 - step))
+
+    def spread(step, low):
+        plane = far_first(step)
+        acts_x_copy(plane, x_lo, low).start()
+        for ahead in FAR_FIRST:
+            acts_y_copy(plane, ahead, low).start()
+
+    def spread_mixed(step):
+        for ahead in range(1, IMAGES):
+            mixed_copy(far_first(step), ahead).start()
+
+    def pass_on(step, low):
+        plane = far_first(step)
+        acts_x_copy(plane, 1 - x_lo, low).wait_recv()
+        for ahead in FAR_FIRST:
+            pass_y_copy(plane, ahead, low).start()
         for ahead in range(1, STACK):
-            acts_y_copy(plane, ahead).start()
-
-    def pass_on(step):
-        plane = around(offset_of(PLANES - 1 - step))
-        acts_x_copy(plane, 1 - x_lo).wait_recv()
+            acts_y_landed(plane, ahead, low).wait_recv()
+        pass_x_copy(plane, x_lo).start()
+
+    def landed(step, low):
+        plane = far_first(step)
         for ahead in range(1, STACK):
-            pass_y_copy(plane, ahead).start()
-        for ahead in range(1, STACK):
-            acts_y_landed(plane, ahead).wait_recv()
-        pass_x_copy(plane, x_lo).start()
+            pass_y_landed(plane, ahead, low).wait_recv()
+        pass_x_copy(plane, 1 - x_lo).wait_recv()
 
     def first_half(step, carry):
-        @pl.when((step >= LAG) & (step < PLANES + LAG))
+        @pl.when(step < PLANES)
+        def _():
+            project(step)
+
+        @pl.when((step >= LAG) & (step < STAGED + LAG))
         def _():
             halfway(step - LAG)
 
-        @pl.when(step == PLANES + LAG - 1)
+        @pl.when(step == STAGED + LAG - 1)
         def _():
             for behind in range(AHEAD):
-                spread(PLANES - 1 - behind)
-
-        @pl.when(step < PLANES)
-        def _():
-            project(step)
+                spread(PLANES - 1 - behind, HEAD)
 
         @pl.when(step >= 2 * LAG)
         def _():
@@ -409,7 +467,12 @@
 
         return carry
 
-    lax.fori_loop(0, PLANES + 2 * LAG, first_half, 0)
+    lax.fori_loop(0, STAGED + 2 * LAG, first_half, 0)
+    for step in range(STAGED, PLANES):
+        collect_straight(step)
+
+    for step in range(SOON):
+        spread(step, HEAD)
 
     whole = strips[...].reshape(BLOCK, 3 * HEAD)
     query_norm = normalize(whole[:, :HEAD]).astype(BF16)
@@ -423,37 +486,45 @@
     mixed = mixed.astype(BF16).reshape(PLANES, STRIP, HEAD)
     for plane in range(PLANES):
         acts[plane, x_lo, y, :, :HEAD] = mixed[plane]
-    for step in range(1, IMAGES):
-        mixed_copy(step).start()
+    for step in range(SOON):
+        spread_mixed(step)
 
     def pair_copy(plane):
         return send(pair_out.at[plane], pair_in.at[plane], pair_sem, (plane,), other_core)
 
-    def ring_copy(step):
-        return send(ring_out.at[step], ring_in.at[step], ring_sem, (step,), plane_device(around(-z_way(step))))
-
-    def ring_landed(step):
-        return send(ring_in.at[step], ring_in.at[step], ring_sem, (step,), plane_device(around(z_way(step))))
-
-    def ring_half_copy(side):
-        rows = pl.ds(32 * side, 32)
+    def ring_way(step, side):
+        return jnp.where(step == 0, 1 - 2 * side, -z_way(step))
+
+    def ring_copy(step, side):
         return send(
-            ring_out.at[0, rows], ring_in.at[0, rows], ring_sem, (7 * side,), plane_device(around(1 - 2 * side))
+            ring_out.at[step, side],
+            ring_in.at[step, side],
+            ring_sem,
+            (step, side),
+            plane_device(around(ring_way(step, side))),
         )
 
-    def ring_half_landed(side):
-        place = ring_in.at[0, pl.ds(32 * side, 32)]
-        return send(place, place, ring_sem, (7 * side,), plane_device(around(2 * side - 1)))
+    def ring_landed(step, side):
+        place = ring_in.at[step, side]
+        return send(place, place, ring_sem, (step, side), plane_device(around(-ring_way(step, side))))
 
     def output(step):
-        plane = around(offset_of(PLANES - 1 - step))
-        for ahead in range(1, STACK):
-            pass_y_landed(plane, ahead).wait_recv()
-        pass_x_copy(plane, 1 - x_lo).wait_recv()
+        plane = far_first(step)
+
+        @pl.when((step < SOON) | (step >= PLANES - AHEAD))
+        def _():
+            landed(step, HEAD)
+            for ahead in range(1, IMAGES):
+                mixed_landed(plane, ahead).wait_recv()
+
+        @pl.when((step >= SOON) & (step < PLANES - AHEAD))
+        def _():
+            landed(step, 0)
+
         rows = jnp.dot(
             from_strips(), acts[plane].reshape(BLOCK, SECOND), preferred_element_type=F32
         ).astype(BF16)
-        block = jnp.dot(rows, second[...], preferred_element_type=F32).reshape(2, 64, WIDTH)
+        block = jnp.dot(rows, second[...], preferred_element_type=F32).reshape(2, 2, 32, WIDTH)
         pair_out[plane] = jnp.where(core == 0, block[1], block[0]).astype(BF16)
         pair_copy(plane).start()
         pair_own[plane] = jnp.where(core == 0, block[0], block[1])
@@ -461,67 +532,54 @@
     def merge(step):
         plane = around(offset_of(PLANES - 1 - step))
         pair_copy(plane).wait_recv()
-        pair_own[plane] = pair_own[plane] + pair_in[plane].astype(F32)
         for side in range(2):
-
-            @pl.when(step == 2 - side)
+            pair_own[plane, side] = pair_own[plane, side] + pair_in[plane, side].astype(F32)
+
+            @pl.when((step >= 3) | (step == 2 - side))
             def _():
-                rows = pl.ds(32 * side, 32)
-                ring_half_landed(side).wait_recv()
-                pair_own[plane, rows] = pair_own[plane, rows] + ring_in[0, rows].astype(F32)
-
-        @pl.when(step >= 3)
-        def _():
-            ring_landed(step - 2).wait_recv()
-            pair_own[plane] = pair_own[plane] + ring_in[step - 2].astype(F32)
-
-        @pl.when(step < PLANES - 1)
-        def _():
-            ring_out[step] = pair_own[plane].astype(BF16)
-
-        @pl.when(step == 0)
-        def _():
-            for side in range(2):
-                ring_half_copy(side).start()
-
-        @pl.when((step > 0) & (step < PLANES - 1))
-        def _():
-            ring_copy(step).start()
+                before = jnp.maximum(step - 2, 0)
+                ring_landed(before, side).wait_recv()
+                pair_own[plane, side] = pair_own[plane, side] + ring_in[before, side].astype(F32)
+
+            @pl.when(step < PLANES - 1)
+            def _():
+                ring_out[step, side] = pair_own[plane, side].astype(BF16)
+                ring_copy(step, side).start()
 
     for copy in weights[8:]:
         copy.wait()
 
     def second_half(step, carry):
-        @pl.when(step < PLANES - AHEAD)
-        def _():
-            spread(step)
-
-        @pl.when(step < AHEAD)
-        def _():
-            pass_on(PLANES - AHEAD + step)
-
-        @pl.when((step >= LAG) & (step < PLANES - AHEAD + LAG))
-        def _():
-            pass_on(step - LAG)
-
-        @pl.when(step == 2 * LAG)
-        def _():
-            for ahead in range(1, IMAGES):
-                mixed_landed(ahead).wait_recv()
-
-        @pl.when(step >= 2 * LAG + 1)
-        def _():
-            merge(step - 2 * LAG - 1)
-
-        @pl.when((step >= 2 * LAG) & (step < PLANES + 2 * LAG))
-        def _():
-            output(step - 2 * LAG)
+        @pl.when(step < PLANES - AHEAD - SOON)
+        def _():
+            spread(step + SOON, 0)
+
+        @pl.when((step >= PLANES - AHEAD - SOON) & (step < PLANES - SOON))
+        def _():
+            spread_mixed(step + SOON)
+
+        @pl.when((step < SOON) | ((step >= PLANES - AHEAD) & (step < PLANES)))
+        def _():
+            pass_on(step, HEAD)
+
+        @pl.when((step >= SOON) & (step < PLANES - AHEAD))
+        def _():
+            pass_on(step, 0)
+
+        @pl.when((step >= SOON) & (step < PLANES + SOON))
+        def _():
+            output(step - SOON)
+
+        @pl.when(step >= SOON + 1)
+        def _():
+            merge(step - SOON - 1)
 
         return carry
 
-    lax.fori_loop(0, PLANES + 2 * LAG + 1, second_half, 0)
-    ring_landed(6).wait_recv()
-    lines[...] = pair_own[z] + ring_in[6].astype(F32)
+    lax.fori_loop(0, PLANES + SOON + 1, second_half, 0)
+    for side in range(2):
+        ring_landed(6, side).wait_recv()
+        lines[pl.ds(32 * side, 32), :] = pair_own[z, side] + ring_in[6, side].astype(F32)
     for side in range(2):
         for image in range(IMAGES):
             final_out[side, image] = lines[pl.ds(side * 32 + image * ROWS, ROWS), :].astype(BF16)
@@ -549,30 +607,45 @@
         total = final_in[block, 0].astype(F32) + final_in[block, 1].astype(F32)
         out[:, columns] = (tokens[:, columns].astype(F32) + total).astype(BF16)
 
-    for step in range(1, IMAGES):
-        mixed_copy(step).wait_send()
+    for step in range(PLANES):
+        plane = far_first(step)
+        low = 0 if SOON <= step < PLANES - AHEAD else HEAD
+        acts_x_copy(plane, x_lo, low).wait_send()
+        for ahead in range(1, STACK):
+            acts_y_copy(plane, ahead, low).wait_send()
+            pass_y_copy(plane, ahead, low).wait_send()
+        if low:
+            for ahead in range(1, IMAGES):
+                mixed_copy(plane, ahead).wait_send()
     for piece in pieces:
         norm_copy(*piece).wait_send()
         final_copy(*piece).wait_send()
     for step in range(1, 7):
         z_copy(step).wait_send()
-        ring_copy(step).wait_send()
     for side in range(2):
         z_half_copy(side).wait_send()
-        ring_half_copy(side).wait_send()
-
-    def sent(plane, carry):
+        for step in range(PLANES - 1):
+            ring_copy(step, side).wait_send()
+
+    def sent(step, carry):
+        plane = around(-offset_of(step))
         core_copy(plane, core).wait_send()
         pair_copy(plane).wait_send()
-        part_x_copy(plane).wait_send()
-        mid_y_copy(plane).wait_send()
-        acts_x_copy(plane, x_lo).wait_send()
         pass_x_copy(plane, x_lo).wait_send()
-        for ahead in range(1, STACK):
-            part_y_copy(plane, ahead).wait_send()
-            mid_x_copy(plane, ahead).wait_send()
-            acts_y_copy(plane, ahead).wait_send()
-            pass_y_copy(plane, ahead).wait_send()
+
+        @pl.when(step < STAGED)
+        def _():
+            part_x_copy(plane).wait_send()
+            mid_y_copy(plane).wait_send()
+            for ahead in range(1, STACK):
+                part_y_copy(plane, ahead).wait_send()
+                mid_x_copy(plane, ahead).wait_send()
+
+        @pl.when(step >= STAGED)
+        def _():
+            for ahead in range(1, IMAGES):
+                straight_copy(step, ahead).wait_send()
+
         return carry
 
     lax.fori_loop(0, PLANES, sent, 0)
@@ -608,13 +681,14 @@
             pltpu.VMEM((PLANES, STRIP, Y_FIRST), BF16),
             pltpu.VMEM((PLANES, STRIP, Y_FIRST), F32),
             pltpu.VMEM((PLANES, STRIP, Y_FIRST), BF16),
+            pltpu.VMEM((STRAIGHT, IMAGES, STRIP, FIRST), BF16),
             pltpu.VMEM((PLANES, STRIP, 3 * HEAD), F32),
             pltpu.VMEM((PLANES, 2, STACK, STRIP, SECOND), BF16),
-            pltpu.VMEM((PLANES, 64, WIDTH), F32),
-            pltpu.VMEM((PLANES, 64, WIDTH), BF16),
-            pltpu.VMEM((PLANES, 64, WIDTH), BF16),
-            pltpu.VMEM((PLANES - 1, 64, WIDTH), BF16),
-            pltpu.VMEM((PLANES - 1, 64, WIDTH), BF16),
+            pltpu.VMEM((PLANES, 2, 32, WIDTH), F32),
+            pltpu.VMEM((PLANES, 2, 32, WIDTH), BF16),
+            pltpu.VMEM((PLANES, 2, 32, WIDTH), BF16),
+            pltpu.VMEM((PLANES - 1, 2, 32, WIDTH), BF16),
+            pltpu.VMEM((PLANES - 1, 2, 32, WIDTH), BF16),
             pltpu.VMEM((2, IMAGES, ROWS, WIDTH), BF16),
             pltpu.VMEM((IMAGES, 2, ROWS, WIDTH), BF16),
             dma((10,)),
@@ -622,10 +696,11 @@
             dma((2, 9)),
             dma((2, PLANES)),
             dma((2, PLANES, 8)),
+            dma((2, STRAIGHT, IMAGES)),
             dma((2, PLANES, 8)),
-            dma((2, IMAGES)),
+            dma((2, PLANES, IMAGES)),
             dma((2, PLANES)),
-            dma((2, PLANES)),
+            dma((2, PLANES - 1, 2)),
             dma((2, IMAGES, 2)),
         ],
         compiler_params=pltpu.CompilerParams(

time: 85.6 us -> 80.7 us (0.943)
  Pallas kernels: 83.2 us -> 78.5 us
    pallas_call x1, Pallas kernels: 83.2 us -> 78.5 us  [per_device(): pl.pallas_call(kernel, out_shape=jax.ShapeDtypeStruct(tokens.shape, BF16)...]
where the time goes in v5:
time: 80.7 us; the launch traced here: 80.6 us
  Pallas kernels  78.5 us (97%)
  local copies, waits for them, and re-layouts  1.44 us (2%)
    pallas_call x1, Pallas kernels, per_device(): pl.pallas_call(kernel, out_shape=jax.ShapeDtypeStruct(tokens.shape, BF16)...  78.5 us

profile of v5, /device:TPU:8, one launch (start us, length us, event | category | flops | bytes accessed | tf_op | source)
XLA Modules:
  0.0 80.6 jit_solution(1288973457951840880)
XLA Ops:
  0.7 78.5 %shard_map.100 = bf16[4,6144]{1,0:T(4,128)(2,1)} custom-call(bf16[4,6144]{1,0:T(4,128)(2,1)} %tokens_hbm.1, f32[1,6144]{1,0:T(1,128)} %bitcast.1, bf16[768,128]{1,0:T(8,128)(2,1)} %w_query.1, bf16[768,128]{1,0:T(8,128)(2,1)} %w_key.1, bf16[768,128]{1,0:T(8,128)(2,1)} %w_value.1, bf16[768,768]{1,0:T(8,128)(2,1)} %w_inner.1, f32[768]{0:T(1024)} %bias_hbm.1, ...), custom_call_target="tpu_custom_call" | custom-call | tf_op jit(solution)/shard_map/pallas_call | solution.py:660
  79.1 1.4 %copy.13 = bf16[4,6144]{1,0:T(4,128)(2,1)} copy(bf16[4,6144]{1,0:T(4,128)(2,1)} %shard_map.100) | data formatting | bytes 98304
